TPU v7x, 32 devices: a whole 2x2x4 slice. The times are simulated.
32 devices in a mesh: row: 4 (over z), col: 8 (over y, x, core).
Axes of the slice: x: 2, y: 2, z: 4, core: 2. Of those that a mesh axis runs over, the one named last changes fastest.
Arguments:
- grad_terms: bfloat16 [8, 2, 4096, 10240], P('col', None, 'row'), may hold values from -25 to 25, as said below
- row_moment: float32 [2, 4096], P(None, 'row'), may hold values from 0.01 to 3
- col_moment: float32 [2, 10240], P(None, 'col'), may hold values from 0.01 to 1
Outputs:
- update: float32 [2, 4096, 10240], P(None, 'row', 'col')
- new_rows: float32 [2, 4096], P(None, 'row')
- new_cols: float32 [2, 10240], P(None, 'col')
Inputs may be any that keep to these rules, and one draw needn't show every extreme that they name: `grad_terms`: partial gradient terms of the 8 batch shards.
All inputs are finite; a program needn't handle non-finite values.
Results may differ from a plain program's by a relative error of at most 0.0003.
Values sent between devices are 32-bit elements; how exact they have to be, the bound alone decides.
No kernel may reach another device: no remote copies, remote signals or barrier semaphores. Data moves between devices by JAX's collectives and lax.ppermute only.
A program may use at most 256 MiB of HBM per device.

v0:
```python
import jax
import jax.numpy as jnp
from jax import lax
from jax.sharding import PartitionSpec as P

D = 4096
FF = 10240


second_decay = 1.0 - 100.0 ** (-0.8)
tiny_square = 1e-30


def on_device(grad_terms, row_moment, col_moment):
    partial_terms = grad_terms[0]
    gradient = lax.psum_scatter(
        partial_terms.astype(jnp.float32), "col", scatter_dimension=2, tiled=True
    )
    squares = gradient * gradient + tiny_square
    row_part = jnp.sum(squares, axis=2)
    col_part = jnp.sum(squares, axis=1)
    row_full = lax.psum(row_part, "col")
    col_full = lax.psum(col_part, "row")
    new_rows = second_decay * row_moment + (1.0 - second_decay) * row_full / FF
    new_cols = second_decay * col_moment + (1.0 - second_decay) * col_full / D
    row_level = lax.psum(jnp.sum(new_rows, axis=1), "row") / D
    estimate = new_rows[:, :, None] * new_cols[:, None, :] / row_level[:, None, None]
    raw_update = gradient / jnp.sqrt(estimate)
    clip_total = lax.psum(jnp.sum(raw_update * raw_update, axis=(1, 2)), ("row", "col"))
    clip_scale = jnp.maximum(1.0, jnp.sqrt(clip_total / (D * FF)))
    update = raw_update / clip_scale[:, None, None]
    return (update, new_rows, new_cols)


def solution(mesh):
    placed = (P("col", None, "row", None), P(None, "row"), P(None, "col"))
    return jax.shard_map(
        on_device,
        mesh=mesh,
        in_specs=placed,
        out_specs=(P(None, "row", "col"), P(None, "row"), P(None, "col")),
        check_vma=False,
    )
```

profile of v0, /device:TPU:10, one launch (start us, length us, event | category | flops | bytes accessed | tf_op | source)
XLA Modules:
  0.0 610.9 jit_solution(3607653950137789142)
XLA Ops:
  7.2 0.0 reduce-scatter.2.cloned.1.call-start
  7.2 40.9 %bitcast_convert_fusion = f32[2,1024,10240]{2,1,0:T(8,128)} fusion(bf16[1,2,1024,10240]{3,2,1,0:T(8,128)(2,1)} %param.3), kind=kLoop, calls=%fused_computation | loop fusion | flops 20971520 | bytes 125829120 | tf_op jit(solution)/shard_map/convert_element_type | solution.py:17
  48.1 0.0 reduce-scatter.2.cloned.1.call-update
  48.1 0.0 copy-start.3
  48.1 0.0 copy-start.2
  48.1 464.0 %reduce-scatter.2.cloned.1.call-done = f32[2,1024,1280]{2,1,0:T(8,128)} async-done(((f32[2,1024,10240]{2,1,0:T(8,128)}), f32[2,1024,1280]{2,1,0:T(8,128)}) %reduce-scatter.2.cloned.1.call-update) | async-done | bytes 10485776 | tf_op jit(solution)/shard_map/reduce_scatter | solution.py:16
  512.1 5.8 fusion
  517.9 10.3 %psum.28 = f32[2,1024]{1,0:T(2,128)S(1)} all-reduce(f32[2,1024]{1,0:T(2,128)S(1)} %get-tuple-element.4), channel_id=1, replica_groups=mesh['row'=4,'col'=8] {'col'}, use_global_device_ids=true, to_apply=%region_2.0 | all-reduce | flops 2048 | bytes 16384 | tf_op jit(solution)/shard_map/psum | solution.py:22
  528.1 0.0 copy-done.3
  528.1 0.1 fusion.2
  528.3 0.0 copy-start.1
  528.3 15.1 %all-reduce = (f32[2]{0:T(128)S(1)}, f32[2,1280]{1,0:T(2,128)S(1)}) all-reduce(f32[2]{0:T(128)S(1)} %get-tuple-element.7, f32[2,1280]{1,0:T(2,128)S(1)} %get-tuple-element.3), channel_id=1, replica_groups=mesh['row'=4,'col'=8] {'row'}, use_global_device_ids=true, to_apply=%region_6.0 | all-reduce | flops 2562 | bytes 20496 | tf_op jit(solution)/shard_map/psum | solution.py:26
  543.4 0.0 copy-done.2
  543.4 0.0 copy-start
  543.4 5.9 multiply_reduce_fusion
  549.4 45.0 %psum.31 = f32[2]{0:T(128)S(1)} all-reduce(f32[2]{0:T(128)S(1)} %multiply_reduce_fusion), channel_id=1, replica_groups=mesh['row'=4,'col'=8] {'row','col'}, use_global_device_ids=true, to_apply=%region_8.0 | all-reduce | flops 2 | bytes 16 | tf_op jit(solution)/shard_map/psum | solution.py:29
  594.4 9.6 %broadcast_divide_fusion = f32[2,1024,1280]{2,1,0:T(8,128)} fusion(f32[2]{0:T(128)S(1)} %sqrt_maximum_fusion, f32[2,1024,1280]{2,1,0:T(8,128)} %reduce-scatter.2.cloned.1.call-done, f32[2]{0:T(128)S(1)} %broadcast_multiply_fusion, f32[2,1280]{1,0:T(2,128)S(1)} %multiply_add_fusion.1, f32[2,1024]{1,0:T(2,128)S(1)} %get-tuple-element.8), kind=kLoop, calls=%fused_computation.6 | loop fusion | flops 10485760 | bytes 20989968 | tf_op jit(solution)/shard_map/div | solution.py:31
  604.0 0.0 copy-done.1
  604.0 0.0 copy-done
  (3 shorter events, 0.0 us)
Async XLA Ops:
  7.2 504.9 %reduce-scatter.2.cloned.1.call-start = ((), (), s32[]{:S(2)}) async-start(), calls=%async_computation.1 | async-start | bytes 94371840 | tf_op jit(solution)/shard_map/reduce_scatter | solution.py:16
  48.1 480.0 %copy-start.3 = (f32[2,1024]{1,0:T(2,128)S(1)}, f32[2,1024]{1,0:T(2,128)}, u32[]{:S(2)}) copy-start(f32[2,1024]{1,0:T(2,128)} %param.4) | copy-start | bytes 24580
  48.1 495.3 %copy-start.2 = (f32[2,1280]{1,0:T(2,128)S(1)}, f32[2,1280]{1,0:T(2,128)}, u32[]{:S(2)}) copy-start(f32[2,1280]{1,0:T(2,128)} %param.5) | copy-start | bytes 30724
  528.3 75.7 %copy-start.1 = (f32[2,1024]{1,0:T(2,128)}, f32[2,1024]{1,0:T(2,128)S(1)}, u32[]{:S(2)}) copy-start(f32[2,1024]{1,0:T(2,128)S(1)} %get-tuple-element.8) | copy-start | bytes 24580
  543.4 60.6 %copy-start = (f32[2,1280]{1,0:T(2,128)}, f32[2,1280]{1,0:T(2,128)S(1)}, u32[]{:S(2)}) copy-start(f32[2,1280]{1,0:T(2,128)S(1)} %multiply_add_fusion.1) | copy-start | bytes 30724
Sparse Core Ops, SparseCore 0:
  48.2 463.8 reduce-scatter.1
where the time goes:
time: 611 us
  waiting for transfers between devices  464 us (76%)
  blocking collectives  70.4 us (12%)
  other arithmetic  62.3 us (10%)
  between operations  14.1 us (2%)
    reduce_scatter x1, waiting for transfers between devices, on_device(): lax.psum_scatter(partial_terms.astype(jnp.float32), 'col', scatter_dimens...  464 us
    psum x1, blocking collectives, on_device(): lax.psum(jnp.sum(raw_update * raw_update, axis=(1, 2)), ('row', 'col'))  45 us
    convert_element_type x1, other arithmetic, on_device(): partial_terms.astype(jnp.float32)  40.9 us
    psum x1, blocking collectives, on_device(): row_level = lax.psum(jnp.sum(new_rows, axis=1), 'row') / D  15.1 us
  transfers between devices with their start and end apart: 1, of which 1 were waited for; matrix products, arithmetic and copies ran while one was open for 0% of the time, Pallas kernels for 0%

commit v1 on v0

v1 whole, which is shorter than its diff:
```python
import jax
import jax.numpy as jnp
from jax import lax
from jax.experimental import pallas as pl
from jax.experimental.pallas import tpu as pltpu
from jax.sharding import PartitionSpec as P


second_decay = 1.0 - 100.0 ** (-0.8)
tiny_square = 1e-30


FIRST = (1, 3, 4, 4, 4)
LAST = (4, 4, 4, 2, 2)
LANES = 128
STEP = 64

ANY = pl.BlockSpec(memory_space=pl.ANY)
ON_CHIP = pl.BlockSpec(memory_space=pltpu.VMEM)
LIMITS = pltpu.CompilerParams(vmem_limit_bytes=24 << 20)


def on_chip(value):
    return pltpu.with_memory_space_constraint(value, pltpu.VMEM)


def in_hbm(value):
    return pltpu.with_memory_space_constraint(value, pltpu.HBM)


def hbm_shape(shape):
    return pltpu.HBM(shape, jnp.float32)


def exchange(value, axis, size, mask):
    return lax.ppermute(value, axis, [(i, i ^ mask) for i in range(size)])


def chip_shape(shape):
    return pltpu.VMEM(shape, jnp.float32)


def added(refs):
    total = refs[0][...]
    for ref in refs[1:]:
        total = total + ref[...]
    return total


def add(parts):
    def body(*refs):
        refs[-1][...] = added(refs[:-1])

    return pl.pallas_call(
        body,
        in_specs=[ON_CHIP] * len(parts),
        out_specs=ON_CHIP,
        out_shape=chip_shape(parts[0].shape),
        compiler_params=LIMITS,
        name="add",
    )(*[on_chip(part) for part in parts])


def sum_over(value, axis, size):
    parts = [value]
    mask = 1
    while mask < size:
        value = parts[0] if len(parts) == 1 else add(parts)
        parts = [value, exchange(value, axis, size, mask)]
        mask *= 2
    return parts


def block_of(start, rows, most):
    return max(
        b for b in range(16, most + 1, 16) if b == 16 or not (rows % b or start % b)
    )


def peer_half(table, terms, token, chunk, places, width):
    matrix, start, rows = chunk
    block = block_of(start, rows, STEP)

    def body(table_ref, *refs):
        out = refs[-1]
        for half in range(2):
            for p in range(places):
                out[half, p] = refs[half * places + p][...].astype(jnp.float32)

    def terms_spec(half, p):
        return pl.BlockSpec(
            (None, None, block, width),
            lambda i, t: (matrix, half, start // block + i, t[half, p] ^ 1),
        )

    specs = [terms_spec(half, p) for half in range(2) for p in range(places)]
    return pl.pallas_call(
        body,
        grid_spec=pltpu.PrefetchScalarGridSpec(
            num_scalar_prefetch=1,
            grid=(rows // block,),
            in_specs=[*specs, ANY],
            out_specs=pl.BlockSpec((2, places, block, width), lambda i, t: (0, 0, i, 0)),
        ),
        out_shape=hbm_shape((2, places, rows, width)),
        compiler_params=LIMITS,
        name="peer_half",
    )(table, *[terms] * len(specs), token)


def partial_sums(table, terms, from_peer, received, token, chunk, base, width):
    matrix, start, rows = chunk
    block = block_of(start, rows, STEP)
    count = len(received)

    def body(table_ref, *refs):
        own, refs = refs[: 2 * base], refs[2 * base :]
        peer, others, outs = refs[0], refs[1 : 1 + 2 * count], refs[-2:]
        for half in range(2):
            for p in range(base):
                total = own[half * base + p][...].astype(jnp.float32) + peer[half, p]
                for k in range(count):
                    total = total + others[2 * k + half][p]
                outs[half][p] = total

    def terms_spec(half, p):
        return pl.BlockSpec(
            (None, None, block, width),
            lambda i, t: (matrix, half, start // block + i, t[half, base + p]),
        )

    specs = [terms_spec(half, p) for half in range(2) for p in range(base)]
    shifted = pl.BlockSpec((base, block, width), lambda i, t: (1, i, 0))
    plain = pl.BlockSpec((base, block, width), lambda i, t: (0, i, 0))
    shape = hbm_shape((base, rows, width))
    return pl.pallas_call(
        body,
        grid_spec=pltpu.PrefetchScalarGridSpec(
            num_scalar_prefetch=1,
            grid=(rows // block,),
            in_specs=[
                *specs,
                pl.BlockSpec((2, base, block, width), lambda i, t: (0, 1, i, 0)),
                *[shifted] * (2 * count),
                ANY,
            ],
            out_specs=[plain, plain],
        ),
        out_shape=[shape, shape],
        compiler_params=LIMITS,
        name="partial_sums",
    )(
        table, *[terms] * len(specs), in_hbm(from_peer),
        *[in_hbm(r) for pair in received for r in pair], token,
    )


def lane_groups(values, width):
    total = values[:, :LANES]
    for c in range(LANES, width, LANES):
        total = total + values[:, c : c + LANES]
    return total


def final_sums(table, terms, from_peer, received, totals, token, chunk, half_rows, width):
    matrix, start, rows = chunk
    block = block_of(start, rows, STEP)
    steps = rows // block
    count = len(received)
    begin = totals is None

    def body(table_ref, own, peer, *refs):
        others = refs[: 2 * count]
        out, row_out, col_out, lanes = refs[-4:]
        i = pl.program_id(0)

        @pl.when(i == 0)
        def _():
            if begin:
                col_out[...] = jnp.zeros_like(col_out)

        for half in range(2):
            total = own[half].astype(jnp.float32) + peer[half]
            for k in range(count):
                total = total + others[2 * k + half][...]
            out[half, pl.ds(pl.multiple_of(start + i * block, 8), block), :] = total
            squares = total * total + tiny_square
            col_out[...] += jnp.sum(squares, axis=0, keepdims=True)
            lanes[half, pl.ds(pl.multiple_of(i * block, block), block), :] = lane_groups(
                squares, width
            )

        @pl.when(i == steps - 1)
        def _():
            for half in range(2):
                row_out[half : half + 1, start : start + rows] = jnp.sum(
                    lanes[half].T, axis=0, keepdims=True
                )

    one = pl.BlockSpec((None, block, width), lambda i, t: (0, i, 0))
    first = 3 + 2 * count
    return pl.pallas_call(
        body,
        grid_spec=pltpu.PrefetchScalarGridSpec(
            num_scalar_prefetch=1,
            grid=(steps,),
            in_specs=[
                pl.BlockSpec(
                    (None, 2, block, width),
                    lambda i, t: (matrix, 0, start // block + i, t[0, 0]),
                ),
                pl.BlockSpec((2, None, block, width), lambda i, t: (0, 0, i, 0)),
                *[one] * (2 * count),
                *([] if begin else [ON_CHIP] * 3),
                ANY,
            ],
            out_specs=[ON_CHIP] * 3,
            scratch_shapes=[pltpu.VMEM((2, rows, LANES), jnp.float32)],
        ),
        out_shape=[
            chip_shape((2, half_rows, width)),
            chip_shape((2, half_rows)),
            chip_shape((1, width)),
        ],
        input_output_aliases={} if begin else {first + k: k for k in range(3)},
        compiler_params=LIMITS,
        name="final_sums",
    )(
        table, terms, in_hbm(from_peer), *[in_hbm(r) for pair in received for r in pair],
        *([] if begin else [on_chip(v) for v in totals]), token,
    )


def down_rows(row):
    return jnp.broadcast_to(row, (LANES, LANES)).T


def over_rows(gradient, row_parts, columns, row_moment, so_far, token, matrix, sizes):
    mats, rows, width, total_cols = sizes
    half_rows = rows // 2
    count = len(row_parts)
    begin = so_far is None

    def body(g, *refs):
        parts, (col, old) = refs[:count], refs[count : count + 2]
        out, moments, message = refs[-3:]
        if begin:
            message[...] = jnp.zeros_like(message)
        message[matrix : matrix + 1, :] = col[...]
        level = jnp.zeros((1, LANES), jnp.float32)
        squares = [jnp.zeros((8, LANES), jnp.float32)] * (width // LANES)
        for b in range(rows // LANES):
            half, first = b * LANES // half_rows, b * LANES % half_rows
            at = slice(first, first + LANES)
            total = parts[0][half : half + 1, at]
            for part in parts[1:]:
                total = total + part[half : half + 1, at]
            whole = slice(b * LANES, (b + 1) * LANES)
            moment = (
                second_decay * old[matrix : matrix + 1, whole]
                + (1.0 - second_decay) * total / total_cols
            )
            moments[matrix : matrix + 1, whole] = moment
            level = level + moment
            factor = down_rows(lax.rsqrt(moment))
            for k in range(width // LANES):
                lane = slice(k * LANES, (k + 1) * LANES)
                scaled = g[half, at, lane] * factor
                out[half, at, lane] = scaled
                squares[k] = squares[k] + jnp.sum(
                    (scaled * scaled).reshape(LANES // 8, 8, LANES), axis=0
                )
        for k in range(width // LANES):
            message[mats + matrix : mats + matrix + 1, k * LANES : (k + 1) * LANES] = jnp.sum(
                squares[k], axis=0, keepdims=True
            )
        message[2 * mats + matrix : 2 * mats + matrix + 1, :LANES] = level

    return pl.pallas_call(
        body,
        in_specs=[ON_CHIP] * (3 + count + (0 if begin else 2)) + [ANY],
        out_specs=[ON_CHIP] * 3,
        out_shape=[
            chip_shape(gradient.shape),
            chip_shape((mats, rows)),
            chip_shape((3 * mats, width)),
        ],
        input_output_aliases={0: 0} if begin else {0: 0, 3 + count: 1, 4 + count: 2},
        compiler_params=LIMITS,
        name="over_rows",
    )(
        *[on_chip(v) for v in (gradient, *row_parts, columns, row_moment)],
        *([] if begin else [on_chip(v) for v in so_far]), token,
    )


def over_columns(parts, col_moment, sizes, total_rows):
    mats, _, width, _ = sizes

    def body(*refs):
        old, new_cols, levels, lanes = refs[len(parts) :]
        both = added(refs[: len(parts)])
        new = second_decay * old[...] + (1.0 - second_decay) * both[:mats] / total_rows
        new_cols[...] = new
        lanes[...] = lane_groups(both[mats : 2 * mats] / new, width)
        levels[...] = jnp.broadcast_to(
            jnp.sum(both[2 * mats :], axis=1, keepdims=True) / total_rows, (mats, LANES)
        )

    return pl.pallas_call(
        body,
        in_specs=[ON_CHIP] * (len(parts) + 1),
        out_specs=[ON_CHIP] * 3,
        out_shape=[
            chip_shape((mats, width)), chip_shape((mats, LANES)), chip_shape((mats, LANES)),
        ],
        compiler_params=LIMITS,
        name="over_columns",
    )(*[on_chip(v) for v in (*parts, col_moment)])


def scale(scaled, new_rows, new_cols, levels, clip_parts, sizes, total_rows):
    mats, rows, width, total_cols = sizes
    half_rows = rows // 2
    block = half_rows // 2
    count = len(clip_parts)

    def body(*refs):
        r, c, level, *parts = refs[mats : mats + 3 + count]
        out, rows_out, cols_out = refs[-3:]
        m, i = pl.program_id(0), pl.program_id(1)

        @pl.when((m == 0) & (i == 0))
        def _():
            rows_out[...] = r[...]
            cols_out[...] = c[...]

        for matrix in range(mats):

            @pl.when(m == matrix)
            def _(matrix=matrix):
                one = slice(matrix, matrix + 1)
                row_level = level[one, :1]
                clip = parts[0][one, :]
                for part in parts[1:]:
                    clip = clip + part[one, :]
                clip = jnp.sum(clip, axis=1, keepdims=True)
                clip = jnp.sqrt(clip * row_level / (total_rows * total_cols))
                factor = lax.rsqrt(c[one, :]) * (jnp.sqrt(row_level) / jnp.maximum(1.0, clip))
                at = pl.ds(pl.multiple_of((i % 2) * block, 8), block)
                out[...] = refs[matrix][i // 2, at, :] * factor

    return pl.pallas_call(
        body,
        grid=(mats, 4),
        in_specs=[ON_CHIP] * (mats + 3 + count),
        out_specs=[
            pl.BlockSpec((None, block, width), lambda m, i: (m, i, 0)),
            pl.BlockSpec((mats, rows), lambda m, i: (0, 0)),
            pl.BlockSpec((mats, width), lambda m, i: (0, 0)),
        ],
        out_shape=[hbm_shape((mats, rows, width)), hbm_shape((mats, rows)), hbm_shape((mats, width))],
        compiler_params=LIMITS,
        name="scale",
    )(*[on_chip(v) for v in (*scaled, new_rows, new_cols, levels, *clip_parts)])


def chunks_of(mats):
    chunks = []
    for matrix in range(mats):
        start = 0
        for size in LAST if matrix == mats - 1 else FIRST:
            chunks.append((matrix, start, size))
            start += size
    return chunks


def kernel_order(count, bits):
    order = [("peer", 0), ("peer", 1)]
    for t in range(-2, count + max(bits, 1)):
        step = [(f"sum{k}", t - k + 1) for k in range(1, bits)]
        step += [("final", t - max(bits - 1, 0))]
        step += [("sum0", t + 2)] if bits else []
        step += [("peer", t + 3)]
        order += [
            (stage, i) for stage, i in step if 0 <= i < count and (stage, i) not in order
        ]
    return order


def on_device(n_row, n_col, grad_terms, row_moment, col_moment):
    _, mats, rows, all_width = grad_terms.shape
    width = all_width // n_col
    half_rows = rows // 2
    bits = n_col.bit_length() - 2
    places = 1 << bits
    total_rows, total_cols = rows * n_row, all_width
    sizes = (mats, rows, width, total_cols)

    me = lax.axis_index("col").astype(jnp.int32)
    terms = grad_terms.reshape(mats, 2, half_rows, all_width)
    orders = (tuple(range(bits)), tuple(reversed(range(bits))))

    def place_mask(order, place):
        return sum(1 << bit for k, bit in enumerate(order) if place >> (bits - 1 - k) & 1)

    masks = [[2 * place_mask(order, p) for p in range(places)] for order in orders]
    table = jnp.bitwise_xor(jnp.array(masks, jnp.int32), me)

    unit = half_rows // 16
    chunks = [(m, start * unit, size * unit) for m, start, size in chunks_of(mats)]
    last_of = {c[0]: i for i, c in enumerate(chunks)}

    from_peer, received = {}, {i: [] for i in range(len(chunks))}
    totals, row_parts, scaled = [None] * mats, [None] * mats, [None] * mats
    so_far = None
    token = in_hbm(terms)

    def divide_rows(matrix):
        nonlocal so_far, token
        gradient, _, columns = totals[matrix]
        scaled[matrix], *so_far = over_rows(
            gradient, row_parts[matrix], columns, row_moment, so_far, token, matrix, sizes
        )
        token = on_chip(so_far[1])

    finished = []
    for stage, i in kernel_order(len(chunks), bits):
        for entry in finished:
            entry[1] -= 1
            if entry[1] == 0:
                divide_rows(entry[0])
        matrix = chunks[i][0]
        if stage == "peer":
            sent = peer_half(table, terms, token, chunks[i], places, width)
        elif stage == "final":
            totals[matrix] = final_sums(
                table, terms, from_peer[i], received[i], totals[matrix], token,
                chunks[i], half_rows, width,
            )
        else:
            k = int(stage[3:])
            sums = partial_sums(
                table, terms, from_peer[i], received[i], token, chunks[i],
                places >> (k + 1), width,
            )
        if stage == "peer":
            token = in_hbm(sent)
            from_peer[i] = exchange(sent, "col", n_col, 1)
        elif stage == "final":
            token = on_chip(totals[matrix][2])
            if i == last_of[matrix]:
                row_parts[matrix] = sum_over(totals[matrix][1], "col", n_col)
                finished.append([matrix, 4 * n_col.bit_length() - 5])
        else:
            token = in_hbm(sums[0])
            received[i].append(
                [exchange(sums[half], "col", n_col, 2 << orders[half][k]) for half in range(2)]
            )
    for matrix in range(mats):
        if scaled[matrix] is None:
            divide_rows(matrix)

    new_rows, message = so_far
    new_cols, levels, lanes = over_columns(
        sum_over(message, "row", n_row), col_moment, sizes, total_rows
    )
    clip_parts = sum_over(lanes, "col", n_col)
    return scale(scaled, new_rows, new_cols, levels, clip_parts, sizes, total_rows)


def solution(mesh):
    n_row, n_col = mesh.shape["row"], mesh.shape["col"]
    placed = (P("col", None, "row", None), P(None, "row"), P(None, "col"))

    def body(*args):
        return on_device(n_row, n_col, *args)

    return jax.shard_map(
        body,
        mesh=mesh,
        in_specs=placed,
        out_specs=(P(None, "row", "col"), P(None, "row"), P(None, "col")),
        check_vma=False,
    )
```

time: 611 us -> 554 us (0.907)
  Pallas kernels: 0 us -> 155 us
  waiting for transfers between devices: 464 us -> 309 us
  blocking collectives: 70.4 us -> 0 us
  other arithmetic: 62.3 us -> 0.69 us
  starting transfers between devices: 0.04 us -> 49.8 us
  local copies, waits for them, and re-layouts: 0.02 us -> 35.9 us
  between operations: 14.1 us -> 1.33 us
    reduce_scatter x1 -> x0, waiting for transfers between devices: 464 us -> none  [on_device(): lax.psum_scatter(partial_terms.astype(jnp.float32), 'col', scatter_dimens...]
    ppermute x0 -> x61, waiting for transfers between devices: none -> 309 us  [exchange(): return lax.ppermute(value, axis, [(i, i ^ mask) for i in range(size)])]
    pallas_call x0 -> x51, Pallas kernels: none -> 155 us  [the longest x20 71.6 us: partial_sums(): pl.pallas_call(body, grid_spec=pltpu.PrefetchScalarGridSpec(num_scalar_pr...]
    psum x3 -> x0, blocking collectives: 70.4 us -> none  [the longest x1 45 us: on_device(): lax.psum(jnp.sum(raw_update * raw_update, axis=(1, 2)), ('row', 'col'))]
    ppermute x0 -> x61, starting transfers between devices: none -> 49.8 us  [exchange(): return lax.ppermute(value, axis, [(i, i ^ mask) for i in range(size)])]
    convert_element_type x1 -> x0, other arithmetic: 40.9 us -> none  [on_device(): partial_terms.astype(jnp.float32)]
    unnamed x8 -> x181, local copies, waits for them, and re-layouts: 0.02 us -> 35.9 us
    reduce_sum x3 -> x0, other arithmetic: 11.8 us -> none  [the longest x1 5.93 us: on_device(): jnp.sum(raw_update * raw_update, axis=(1, 2))]
  transfers between devices with their start and end apart: 1 -> 61, of which waited for: 1 -> 34; matrix products, arithmetic and copies ran while one was open for 0% -> 0% of each run, Pallas kernels for 0% -> 12%
where the time goes in v1:
time: 554 us; the launch traced here: 551 us
  waiting for transfers between devices  309 us (56%)
  Pallas kernels  155 us (28%)
  starting transfers between devices  49.8 us (9%)
  local copies, waits for them, and re-layouts  35.9 us (6%)
    ppermute x61, waiting for transfers between devices, exchange(): return lax.ppermute(value, axis, [(i, i ^ mask) for i in range(size)])  309 us
    pallas_call x20, Pallas kernels, partial_sums(): pl.pallas_call(body, grid_spec=pltpu.PrefetchScalarGridSpec(num_scalar_pr...  71.6 us
    ppermute x61, starting transfers between devices, exchange(): return lax.ppermute(value, axis, [(i, i ^ mask) for i in range(size)])  49.8 us
    pallas_call x10, Pallas kernels, peer_half(): pl.pallas_call(body, grid_spec=pltpu.PrefetchScalarGridSpec(num_scalar_pr...  43.6 us
    unnamed x181, local copies, waits for them, and re-layouts  35.9 us
    pallas_call x10, Pallas kernels, final_sums(): pl.pallas_call(body, grid_spec=pltpu.PrefetchScalarGridSpec(num_scalar_pr...  30.4 us
  transfers between devices with their start and end apart: 61, of which 34 were waited for; matrix products, arithmetic and copies ran while one was open for 0% of the time, Pallas kernels for 12%

profile of v1, /device:TPU:10, one launch (start us, length us, event | category | flops | bytes accessed | tf_op | source)
XLA Modules:
  0.0 551.2 jit_solution(5741134423484515897)
XLA Ops:
  4.2 4.8 peer_half.11.refs_5_
  9.5 8.4 %collective-permute-done.1.refs_4_.refs_2_.peer = f32[2,4,32,1280]{3,2,1,0:T(8,128)S(1)} collective-permute-done((f32[2,4,32,1280]{3,2,1,0:T(8,128)S(1)}, f32[2,4,32,1280]{3,2,1,0:T(8,128)S(1)}, u32[]{:S(2)}, u32[]{:S(2)}) %collective-permute-start.1) | collective-permute-done | bytes 1310752 | tf_op jit(solution)/shard_map/ppermute | solution.py:36
  23.6 4.5 partial_sums.21
  28.1 4.5 peer_half.12.refs_5_
  34.9 7.9 %collective-permute-done.4.refs_4_.refs_1_ = f32[2,32,1280]{2,1,0:T(8,128)S(1)} collective-permute-done((f32[2,32,1280]{2,1,0:T(8,128)S(1)}, f32[2,32,1280]{2,1,0:T(8,128)S(1)}, u32[]{:S(2)}, u32[]{:S(2)}) %collective-permute-start.4) | collective-permute-done | bytes 327712 | tf_op jit(solution)/shard_map/ppermute | solution.py:36
  49.6 4.0 partial_sums.23
  53.7 4.6 peer_half.13.refs_5_
  62.4 20.6 %collective-permute-done.9.refs_4_.refs_1_ = f32[2,96,1280]{2,1,0:T(8,128)S(1)} collective-permute-done((f32[2,96,1280]{2,1,0:T(8,128)S(1)}, f32[2,96,1280]{2,1,0:T(8,128)S(1)}, u32[]{:S(2)}, u32[]{:S(2)}) %collective-permute-start.9) | collective-permute-done | bytes 983072 | tf_op jit(solution)/shard_map/ppermute | solution.py:36
  84.9 4.0 partial_sums.24
  94.0 4.0 partial_sums.25
  98.0 4.8 peer_half.14.refs_5_
  107.0 27.6 %collective-permute-done.14.refs_4_.refs_1_ = f32[2,128,1280]{2,1,0:T(8,128)S(1)} collective-permute-done((f32[2,128,1280]{2,1,0:T(8,128)S(1)}, f32[2,128,1280]{2,1,0:T(8,128)S(1)}, u32[]{:S(2)}, u32[]{:S(2)}) %collective-permute-start.14) | collective-permute-done | bytes 1310752 | tf_op jit(solution)/shard_map/ppermute | solution.py:36
  140.2 5.1 collective-permute-done.12.refs_3_
  152.2 4.0 partial_sums.27
  156.3 4.8 peer_half.15.refs_5_
  165.2 27.6 %collective-permute-done.21.refs_4_.refs_1_ = f32[2,128,1280]{2,1,0:T(8,128)S(1)} collective-permute-done((f32[2,128,1280]{2,1,0:T(8,128)S(1)}, f32[2,128,1280]{2,1,0:T(8,128)S(1)}, u32[]{:S(2)}, u32[]{:S(2)}) %collective-permute-start.21) | collective-permute-done | bytes 1310752 | tf_op jit(solution)/shard_map/ppermute | solution.py:36
  198.4 8.6 %collective-permute-done.19.refs_3_ = f32[1,128,1280]{2,1,0:T(8,128)S(1)} collective-permute-done((f32[1,128,1280]{2,1,0:T(8,128)S(1)}, f32[1,128,1280]{2,1,0:T(8,128)S(1)}, u32[]{:S(2)}, u32[]{:S(2)}) %collective-permute-start.19) | collective-permute-done | bytes 655392 | tf_op jit(solution)/shard_map/ppermute | solution.py:36
  213.8 4.0 partial_sums.29
  217.8 4.7 peer_half.16.refs_5_
  226.7 27.6 %collective-permute-done.16.refs_4_.refs_1_ = f32[2,128,1280]{2,1,0:T(8,128)S(1)} collective-permute-done((f32[2,128,1280]{2,1,0:T(8,128)S(1)}, f32[2,128,1280]{2,1,0:T(8,128)S(1)}, u32[]{:S(2)}, u32[]{:S(2)}) %collective-permute-start.16) | collective-permute-done | bytes 1310752 | tf_op jit(solution)/shard_map/ppermute | solution.py:36
  259.9 8.7 %collective-permute-done.25.refs_3_ = f32[1,128,1280]{2,1,0:T(8,128)S(1)} collective-permute-done((f32[1,128,1280]{2,1,0:T(8,128)S(1)}, f32[1,128,1280]{2,1,0:T(8,128)S(1)}, u32[]{:S(2)}, u32[]{:S(2)}) %collective-permute-start.25) | collective-permute-done | bytes 655392 | tf_op jit(solution)/shard_map/ppermute | solution.py:36
  275.3 4.1 partial_sums.31
  279.3 4.7 peer_half.17.refs_5_
  288.2 27.6 %collective-permute-done.27.refs_4_.refs_1_ = f32[2,128,1280]{2,1,0:T(8,128)S(1)} collective-permute-done((f32[2,128,1280]{2,1,0:T(8,128)S(1)}, f32[2,128,1280]{2,1,0:T(8,128)S(1)}, u32[]{:S(2)}, u32[]{:S(2)}) %collective-permute-start.27) | collective-permute-done | bytes 1310752 | tf_op jit(solution)/shard_map/ppermute | solution.py:36
  321.4 8.6 %collective-permute-done.23.refs_3_ = f32[1,128,1280]{2,1,0:T(8,128)S(1)} collective-permute-done((f32[1,128,1280]{2,1,0:T(8,128)S(1)}, f32[1,128,1280]{2,1,0:T(8,128)S(1)}, u32[]{:S(2)}, u32[]{:S(2)}) %collective-permute-start.23) | collective-permute-done | bytes 655392 | tf_op jit(solution)/shard_map/ppermute | solution.py:36
  336.8 4.4 partial_sums.33
  349.2 27.6 %collective-permute-done.37.refs_4_.refs_1_ = f32[2,128,1280]{2,1,0:T(8,128)S(1)} collective-permute-done((f32[2,128,1280]{2,1,0:T(8,128)S(1)}, f32[2,128,1280]{2,1,0:T(8,128)S(1)}, u32[]{:S(2)}, u32[]{:S(2)}) %collective-permute-start.37) | collective-permute-done | bytes 1310752 | tf_op jit(solution)/shard_map/ppermute | solution.py:36
  382.5 8.6 %collective-permute-done.35.refs_3_ = f32[1,128,1280]{2,1,0:T(8,128)S(1)} collective-permute-done((f32[1,128,1280]{2,1,0:T(8,128)S(1)}, f32[1,128,1280]{2,1,0:T(8,128)S(1)}, u32[]{:S(2)}, u32[]{:S(2)}) %collective-permute-start.35) | collective-permute-done | bytes 655392 | tf_op jit(solution)/shard_map/ppermute | solution.py:36
  400.5 3.9 peer_half.19.refs_5_
  410.5 39.8 %collective-permute-done.42.refs_3_ = f32[1,128,1280]{2,1,0:T(8,128)S(1)} collective-permute-done((f32[1,128,1280]{2,1,0:T(8,128)S(1)}, f32[1,128,1280]{2,1,0:T(8,128)S(1)}, u32[]{:S(2)}, u32[]{:S(2)}) %collective-permute-start.42) | collective-permute-done | bytes 655392 | tf_op jit(solution)/shard_map/ppermute | solution.py:36
  474.8 19.7 %collective-permute-done.31.refs_1_ = f32[2,512]{1,0:T(2,128)S(1)} collective-permute-done((f32[2,512]{1,0:T(2,128)S(1)}, f32[2,512]{1,0:T(2,128)S(1)}, u32[]{:S(2)}, u32[]{:S(2)}) %collective-permute-start.31) | collective-permute-done | bytes 4128 | tf_op jit(solution)/shard_map/ppermute | solution.py:36
  545.5 5.7 %scale.1 = (f32[2,1024,1280]{2,1,0:T(8,128)}, f32[2,1024]{1,0:T(2,128)}, f32[2,1280]{1,0:T(2,128)}) custom-call(f32[2,512,1280]{2,1,0:T(8,128)S(1)} %get-tuple-element.136.refs_0_, f32[2,512,1280]{2,1,0:T(8,128)S(1)} %get-tuple-element.155.refs_1_, f32[2,1024]{1,0:T(2,128)S(1)} %get-tuple-element.156.refs_2_, f32[2,1280]{1,0:T(2,128)S(1)} %get-tuple-element.158.refs_3_, ...), custom_call_target="tpu_custom_call" | custom-call | tf_op jit(solution)/shard_map/scale/pallas_call | solution.py:353
  (324 shorter events, 200.3 us)
Async XLA Ops:
  58.2 33.5 %collective-permute-start.5 = (f32[2,4,128,1280]{3,2,1,0:T(8,128)}, f32[2,4,128,1280]{3,2,1,0:T(8,128)S(1)}, u32[]{:S(2)}, u32[]{:S(2)}) collective-permute-start(f32[2,4,128,1280]{3,2,1,0:T(8,128)} %peer_half.13.refs_5_), channel_id=1, source_target_pairs={{0,1},{1,0},{2,3},{3,2},{4,5},{5,4},{6,7},{7,6},{8,9},{9,8},{10,11... | collective-permute-start | bytes 15728648 | tf_op jit(solution)/shard_map/ppermute | solution.py:36
  102.8 47.0 %collective-permute-start.10 = (f32[2,4,128,1280]{3,2,1,0:T(8,128)}, f32[2,4,128,1280]{3,2,1,0:T(8,128)S(1)}, u32[]{:S(2)}, u32[]{:S(2)}) collective-permute-start(f32[2,4,128,1280]{3,2,1,0:T(8,128)} %peer_half.14.refs_5_), channel_id=1, source_target_pairs={{0,1},{1,0},{2,3},{3,2},{4,5},{5,4},{6,7},{7,6},{8,9},{9,8},{10,11... | collective-permute-start | bytes 15728648 | tf_op jit(solution)/shard_map/ppermute | solution.py:36
  102.8 31.7 %collective-permute-start.14 = (f32[2,128,1280]{2,1,0:T(8,128)S(1)}, f32[2,128,1280]{2,1,0:T(8,128)S(1)}, u32[]{:S(2)}, u32[]{:S(2)}) collective-permute-start(f32[2,128,1280]{2,1,0:T(8,128)S(1)} %copy-done.76), channel_id=1, source_target_pairs={{0,4},{1,5},{2,6},{3,7},{4,0},{5,1},{6,2},{7,3},{8,12},{9,13},{10,... | collective-permute-start | bytes 3932168 | tf_op jit(solution)/shard_map/ppermute | solution.py:36
  103.9 31.7 %collective-permute-start.13 = (f32[2,128,1280]{2,1,0:T(8,128)S(1)}, f32[2,128,1280]{2,1,0:T(8,128)S(1)}, u32[]{:S(2)}, u32[]{:S(2)}) collective-permute-start(f32[2,128,1280]{2,1,0:T(8,128)S(1)} %copy-done.39), channel_id=1, source_target_pairs={{0,2},{1,3},{2,0},{3,1},{4,6},{5,7},{6,4},{7,5},{8,10},{9,11},{10,... | collective-permute-start | bytes 3932168 | tf_op jit(solution)/shard_map/ppermute | solution.py:36
  104.5 40.8 %collective-permute-start.12 = (f32[1,96,1280]{2,1,0:T(8,128)S(1)}, f32[1,96,1280]{2,1,0:T(8,128)S(1)}, u32[]{:S(2)}, u32[]{:S(2)}) collective-permute-start(f32[1,96,1280]{2,1,0:T(8,128)S(1)} %copy-done.84), channel_id=1, source_target_pairs={{0,2},{1,3},{2,0},{3,1},{4,6},{5,7},{6,4},{7,5},{8,10},{9,11},{10,... | collective-permute-start | bytes 1474568 | tf_op jit(solution)/shard_map/ppermute | solution.py:36
  106.0 39.3 %collective-permute-start.11 = (f32[1,96,1280]{2,1,0:T(8,128)S(1)}, f32[1,96,1280]{2,1,0:T(8,128)S(1)}, u32[]{:S(2)}, u32[]{:S(2)}) collective-permute-start(f32[1,96,1280]{2,1,0:T(8,128)S(1)} %copy-done.60), channel_id=1, source_target_pairs={{0,4},{1,5},{2,6},{3,7},{4,0},{5,1},{6,2},{7,3},{8,12},{9,13},{10,... | collective-permute-start | bytes 1474568 | tf_op jit(solution)/shard_map/ppermute | solution.py:36
  161.1 50.3 %collective-permute-start.17 = (f32[2,4,128,1280]{3,2,1,0:T(8,128)}, f32[2,4,128,1280]{3,2,1,0:T(8,128)S(1)}, u32[]{:S(2)}, u32[]{:S(2)}) collective-permute-start(f32[2,4,128,1280]{3,2,1,0:T(8,128)} %peer_half.15.refs_5_), channel_id=1, source_target_pairs={{0,1},{1,0},{2,3},{3,2},{4,5},{5,4},{6,7},{7,6},{8,9},{9,8},{10,11... | collective-permute-start | bytes 15728648 | tf_op jit(solution)/shard_map/ppermute | solution.py:36
  161.1 31.7 %collective-permute-start.21 = (f32[2,128,1280]{2,1,0:T(8,128)S(1)}, f32[2,128,1280]{2,1,0:T(8,128)S(1)}, u32[]{:S(2)}, u32[]{:S(2)}) collective-permute-start(f32[2,128,1280]{2,1,0:T(8,128)S(1)} %copy-done.72), channel_id=1, source_target_pairs={{0,4},{1,5},{2,6},{3,7},{4,0},{5,1},{6,2},{7,3},{8,12},{9,13},{10,... | collective-permute-start | bytes 3932168 | tf_op jit(solution)/shard_map/ppermute | solution.py:36
  162.2 31.7 %collective-permute-start.20 = (f32[2,128,1280]{2,1,0:T(8,128)S(1)}, f32[2,128,1280]{2,1,0:T(8,128)S(1)}, u32[]{:S(2)}, u32[]{:S(2)}) collective-permute-start(f32[2,128,1280]{2,1,0:T(8,128)S(1)} %copy-done.35), channel_id=1, source_target_pairs={{0,2},{1,3},{2,0},{3,1},{4,6},{5,7},{6,4},{7,5},{8,10},{9,11},{10,... | collective-permute-start | bytes 3932168 | tf_op jit(solution)/shard_map/ppermute | solution.py:36
  162.7 44.3 %collective-permute-start.19 = (f32[1,128,1280]{2,1,0:T(8,128)S(1)}, f32[1,128,1280]{2,1,0:T(8,128)S(1)}, u32[]{:S(2)}, u32[]{:S(2)}) collective-permute-start(f32[1,128,1280]{2,1,0:T(8,128)S(1)} %copy-done.79), channel_id=1, source_target_pairs={{0,2},{1,3},{2,0},{3,1},{4,6},{5,7},{6,4},{7,5},{8,10},{9,11},{10,... | collective-permute-start | bytes 1966088 | tf_op jit(solution)/shard_map/ppermute | solution.py:36
  164.2 42.9 %collective-permute-start.18 = (f32[1,128,1280]{2,1,0:T(8,128)S(1)}, f32[1,128,1280]{2,1,0:T(8,128)S(1)}, u32[]{:S(2)}, u32[]{:S(2)}) collective-permute-start(f32[1,128,1280]{2,1,0:T(8,128)S(1)} %copy-done.57), channel_id=1, source_target_pairs={{0,4},{1,5},{2,6},{3,7},{4,0},{5,1},{6,2},{7,3},{8,12},{9,13},{10,... | collective-permute-start | bytes 1966088 | tf_op jit(solution)/shard_map/ppermute | solution.py:36
  222.6 50.4 %collective-permute-start.28 = (f32[2,4,128,1280]{3,2,1,0:T(8,128)}, f32[2,4,128,1280]{3,2,1,0:T(8,128)S(1)}, u32[]{:S(2)}, u32[]{:S(2)}) collective-permute-start(f32[2,4,128,1280]{3,2,1,0:T(8,128)} %peer_half.16.refs_5_), channel_id=1, source_target_pairs={{0,1},{1,0},{2,3},{3,2},{4,5},{5,4},{6,7},{7,6},{8,9},{9,8},{10,11... | collective-permute-start | bytes 15728648 | tf_op jit(solution)/shard_map/ppermute | solution.py:36
  222.6 31.7 %collective-permute-start.16 = (f32[2,128,1280]{2,1,0:T(8,128)S(1)}, f32[2,128,1280]{2,1,0:T(8,128)S(1)}, u32[]{:S(2)}, u32[]{:S(2)}) collective-permute-start(f32[2,128,1280]{2,1,0:T(8,128)S(1)} %copy-done.73), channel_id=1, source_target_pairs={{0,4},{1,5},{2,6},{3,7},{4,0},{5,1},{6,2},{7,3},{8,12},{9,13},{10,... | collective-permute-start | bytes 3932168 | tf_op jit(solution)/shard_map/ppermute | solution.py:36
  224.2 44.3 %collective-permute-start.25 = (f32[1,128,1280]{2,1,0:T(8,128)S(1)}, f32[1,128,1280]{2,1,0:T(8,128)S(1)}, u32[]{:S(2)}, u32[]{:S(2)}) collective-permute-start(f32[1,128,1280]{2,1,0:T(8,128)S(1)} %copy-done.80), channel_id=1, source_target_pairs={{0,2},{1,3},{2,0},{3,1},{4,6},{5,7},{6,4},{7,5},{8,10},{9,11},{10,... | collective-permute-start | bytes 1966088 | tf_op jit(solution)/shard_map/ppermute | solution.py:36
  225.7 42.9 %collective-permute-start.24 = (f32[1,128,1280]{2,1,0:T(8,128)S(1)}, f32[1,128,1280]{2,1,0:T(8,128)S(1)}, u32[]{:S(2)}, u32[]{:S(2)}) collective-permute-start(f32[1,128,1280]{2,1,0:T(8,128)S(1)} %copy-done.43), channel_id=1, source_target_pairs={{0,4},{1,5},{2,6},{3,7},{4,0},{5,1},{6,2},{7,3},{8,12},{9,13},{10,... | collective-permute-start | bytes 1966088 | tf_op jit(solution)/shard_map/ppermute | solution.py:36
  284.1 50.3 %collective-permute-start.32 = (f32[2,4,128,1280]{3,2,1,0:T(8,128)}, f32[2,4,128,1280]{3,2,1,0:T(8,128)S(1)}, u32[]{:S(2)}, u32[]{:S(2)}) collective-permute-start(f32[2,4,128,1280]{3,2,1,0:T(8,128)} %peer_half.17.refs_5_), channel_id=1, source_target_pairs={{0,1},{1,0},{2,3},{3,2},{4,5},{5,4},{6,7},{7,6},{8,9},{9,8},{10,11... | collective-permute-start | bytes 15728648 | tf_op jit(solution)/shard_map/ppermute | solution.py:36
  284.1 31.7 %collective-permute-start.27 = (f32[2,128,1280]{2,1,0:T(8,128)S(1)}, f32[2,128,1280]{2,1,0:T(8,128)S(1)}, u32[]{:S(2)}, u32[]{:S(2)}) collective-permute-start(f32[2,128,1280]{2,1,0:T(8,128)S(1)} %copy-done.74), channel_id=1, source_target_pairs={{0,4},{1,5},{2,6},{3,7},{4,0},{5,1},{6,2},{7,3},{8,12},{9,13},{10,... | collective-permute-start | bytes 3932168 | tf_op jit(solution)/shard_map/ppermute | solution.py:36
  285.7 44.3 %collective-permute-start.23 = (f32[1,128,1280]{2,1,0:T(8,128)S(1)}, f32[1,128,1280]{2,1,0:T(8,128)S(1)}, u32[]{:S(2)}, u32[]{:S(2)}) collective-permute-start(f32[1,128,1280]{2,1,0:T(8,128)S(1)} %copy-done.81), channel_id=1, source_target_pairs={{0,2},{1,3},{2,0},{3,1},{4,6},{5,7},{6,4},{7,5},{8,10},{9,11},{10,... | collective-permute-start | bytes 1966088 | tf_op jit(solution)/shard_map/ppermute | solution.py:36
  287.2 42.9 %collective-permute-start.22 = (f32[1,128,1280]{2,1,0:T(8,128)S(1)}, f32[1,128,1280]{2,1,0:T(8,128)S(1)}, u32[]{:S(2)}, u32[]{:S(2)}) collective-permute-start(f32[1,128,1280]{2,1,0:T(8,128)S(1)} %copy-done.44), channel_id=1, source_target_pairs={{0,4},{1,5},{2,6},{3,7},{4,0},{5,1},{6,2},{7,3},{8,12},{9,13},{10,... | collective-permute-start | bytes 1966088 | tf_op jit(solution)/shard_map/ppermute | solution.py:36
  345.1 50.5 %collective-permute-start.33 = (f32[2,4,64,1280]{3,2,1,0:T(8,128)}, f32[2,4,64,1280]{3,2,1,0:T(8,128)S(1)}, u32[]{:S(2)}, u32[]{:S(2)}) collective-permute-start(f32[2,4,64,1280]{3,2,1,0:T(8,128)} %peer_half.18.refs_5_), channel_id=1, source_target_pairs={{0,1},{1,0},{2,3},{3,2},{4,5},{5,4},{6,7},{7,6},{8,9},{9,8},{10,11... | collective-permute-start | bytes 7864328 | tf_op jit(solution)/shard_map/ppermute | solution.py:36
  345.1 31.7 %collective-permute-start.37 = (f32[2,128,1280]{2,1,0:T(8,128)S(1)}, f32[2,128,1280]{2,1,0:T(8,128)S(1)}, u32[]{:S(2)}, u32[]{:S(2)}) collective-permute-start(f32[2,128,1280]{2,1,0:T(8,128)S(1)} %copy-done.75), channel_id=1, source_target_pairs={{0,4},{1,5},{2,6},{3,7},{4,0},{5,1},{6,2},{7,3},{8,12},{9,13},{10,... | collective-permute-start | bytes 3932168 | tf_op jit(solution)/shard_map/ppermute | solution.py:36
  346.7 44.3 %collective-permute-start.35 = (f32[1,128,1280]{2,1,0:T(8,128)S(1)}, f32[1,128,1280]{2,1,0:T(8,128)S(1)}, u32[]{:S(2)}, u32[]{:S(2)}) collective-permute-start(f32[1,128,1280]{2,1,0:T(8,128)S(1)} %copy-done.82), channel_id=1, source_target_pairs={{0,2},{1,3},{2,0},{3,1},{4,6},{5,7},{6,4},{7,5},{8,10},{9,11},{10,... | collective-permute-start | bytes 1966088 | tf_op jit(solution)/shard_map/ppermute | solution.py:36
  348.2 42.9 %collective-permute-start.34 = (f32[1,128,1280]{2,1,0:T(8,128)S(1)}, f32[1,128,1280]{2,1,0:T(8,128)S(1)}, u32[]{:S(2)}, u32[]{:S(2)}) collective-permute-start(f32[1,128,1280]{2,1,0:T(8,128)S(1)} %copy-done.45), channel_id=1, source_target_pairs={{0,4},{1,5},{2,6},{3,7},{4,0},{5,1},{6,2},{7,3},{8,12},{9,13},{10,... | collective-permute-start | bytes 1966088 | tf_op jit(solution)/shard_map/ppermute | solution.py:36
  404.4 57.0 %collective-permute-start.40 = (f32[2,4,64,1280]{3,2,1,0:T(8,128)}, f32[2,4,64,1280]{3,2,1,0:T(8,128)S(1)}, u32[]{:S(2)}, u32[]{:S(2)}) collective-permute-start(f32[2,4,64,1280]{3,2,1,0:T(8,128)} %peer_half.19.refs_5_), channel_id=1, source_target_pairs={{0,1},{1,0},{2,3},{3,2},{4,5},{5,4},{6,7},{7,6},{8,9},{9,8},{10,11... | collective-permute-start | bytes 7864328 | tf_op jit(solution)/shard_map/ppermute | solution.py:36
  404.4 47.0 %collective-permute-start.44 = (f32[2,128,1280]{2,1,0:T(8,128)S(1)}, f32[2,128,1280]{2,1,0:T(8,128)S(1)}, u32[]{:S(2)}, u32[]{:S(2)}) collective-permute-start(f32[2,128,1280]{2,1,0:T(8,128)S(1)} %copy-done.71), channel_id=1, source_target_pairs={{0,4},{1,5},{2,6},{3,7},{4,0},{5,1},{6,2},{7,3},{8,12},{9,13},{10,... | collective-permute-start | bytes 3932168 | tf_op jit(solution)/shard_map/ppermute | solution.py:36
  405.4 46.5 %collective-permute-start.43 = (f32[2,128,1280]{2,1,0:T(8,128)S(1)}, f32[2,128,1280]{2,1,0:T(8,128)S(1)}, u32[]{:S(2)}, u32[]{:S(2)}) collective-permute-start(f32[2,128,1280]{2,1,0:T(8,128)S(1)} %copy-done.34), channel_id=1, source_target_pairs={{0,2},{1,3},{2,0},{3,1},{4,6},{5,7},{6,4},{7,5},{8,10},{9,11},{10,... | collective-permute-start | bytes 3932168 | tf_op jit(solution)/shard_map/ppermute | solution.py:36
  406.0 44.3 %collective-permute-start.42 = (f32[1,128,1280]{2,1,0:T(8,128)S(1)}, f32[1,128,1280]{2,1,0:T(8,128)S(1)}, u32[]{:S(2)}, u32[]{:S(2)}) collective-permute-start(f32[1,128,1280]{2,1,0:T(8,128)S(1)} %copy-done.83), channel_id=1, source_target_pairs={{0,2},{1,3},{2,0},{3,1},{4,6},{5,7},{6,4},{7,5},{8,10},{9,11},{10,... | collective-permute-start | bytes 1966088 | tf_op jit(solution)/shard_map/ppermute | solution.py:36
  409.5 47.5 %collective-permute-start.41 = (f32[1,128,1280]{2,1,0:T(8,128)S(1)}, f32[1,128,1280]{2,1,0:T(8,128)S(1)}, u32[]{:S(2)}, u32[]{:S(2)}) collective-permute-start(f32[1,128,1280]{2,1,0:T(8,128)S(1)} %copy-done.55), channel_id=1, source_target_pairs={{0,4},{1,5},{2,6},{3,7},{4,0},{5,1},{6,2},{7,3},{8,12},{9,13},{10,... | collective-permute-start | bytes 1966088 | tf_op jit(solution)/shard_map/ppermute | solution.py:36
  457.0 40.1 %collective-permute-start.48 = (f32[1,128,1280]{2,1,0:T(8,128)}, f32[1,128,1280]{2,1,0:T(8,128)S(1)}, u32[]{:S(2)}, u32[]{:S(2)}) collective-permute-start(f32[1,128,1280]{2,1,0:T(8,128)} %get-tuple-element.138), channel_id=1, source_target_pairs={{0,2},{1,3},{2,0},{3,1},{4,6},{5,7},{6,4},{7,5},{8,10},{9,11},{10,... | collective-permute-start | bytes 1966088 | tf_op jit(solution)/shard_map/ppermute | solution.py:36
  461.4 36.3 %collective-permute-start.47 = (f32[1,128,1280]{2,1,0:T(8,128)S(1)}, f32[1,128,1280]{2,1,0:T(8,128)S(1)}, u32[]{:S(2)}, u32[]{:S(2)}) collective-permute-start(f32[1,128,1280]{2,1,0:T(8,128)S(1)} %copy-done.42), channel_id=1, source_target_pairs={{0,4},{1,5},{2,6},{3,7},{4,0},{5,1},{6,2},{7,3},{8,12},{9,13},{10,... | collective-permute-start | bytes 1966088 | tf_op jit(solution)/shard_map/ppermute | solution.py:36
  469.1 32.7 %collective-permute-start.46 = (f32[2,64,1280]{2,1,0:T(8,128)}, f32[2,64,1280]{2,1,0:T(8,128)S(1)}, u32[]{:S(2)}, u32[]{:S(2)}) collective-permute-start(f32[2,64,1280]{2,1,0:T(8,128)} %get-tuple-element.137), channel_id=1, source_target_pairs={{0,4},{1,5},{2,6},{3,7},{4,0},{5,1},{6,2},{7,3},{8,12},{9,13},{10,... | collective-permute-start | bytes 1966088 | tf_op jit(solution)/shard_map/ppermute | solution.py:36
  470.1 31.7 %collective-permute-start.45 = (f32[2,64,1280]{2,1,0:T(8,128)}, f32[2,64,1280]{2,1,0:T(8,128)S(1)}, u32[]{:S(2)}, u32[]{:S(2)}) collective-permute-start(f32[2,64,1280]{2,1,0:T(8,128)} %get-tuple-element.134.refs_5_), channel_id=1, source_target_pairs={{0,2},{1,3},{2,0},{3,1},{4,6},{5,7},{6,4},{7,5},{8,10},{9,11},{10,... | collective-permute-start | bytes 1966088 | tf_op jit(solution)/shard_map/ppermute | solution.py:36
  (119 other events, 854.1 us)

commit v2 on v1

v2 whole, which is shorter than its diff:
```python
import jax
import jax.numpy as jnp
from jax import lax
from jax.experimental import pallas as pl
from jax.experimental.pallas import tpu as pltpu
from jax.sharding import PartitionSpec as P


second_decay = 1.0 - 100.0 ** (-0.8)
tiny_square = 1e-30


FIRST = (1, 3, 4, 4, 4)
LAST = (4, 4, 4, 2, 2)
LANES = 128
ON_CHIP_CHUNKS = (0, 1, -1)
STEP = 64

ANY = pl.BlockSpec(memory_space=pl.ANY)
ON_CHIP = pl.BlockSpec(memory_space=pltpu.VMEM)
LIMITS = pltpu.CompilerParams(vmem_limit_bytes=24 << 20)


def on_chip(value):
    return pltpu.with_memory_space_constraint(value, pltpu.VMEM)


def in_hbm(value):
    return pltpu.with_memory_space_constraint(value, pltpu.HBM)


def hbm_shape(shape):
    return pltpu.HBM(shape, jnp.float32)


def exchange(value, axis, size, mask):
    return lax.ppermute(value, axis, [(i, i ^ mask) for i in range(size)])


def chip_shape(shape):
    return pltpu.VMEM(shape, jnp.float32)


def added(values):
    values = list(values)
    while len(values) > 1:
        values = [a + b for a, b in zip(values[::2], values[1::2])]
    return values[0]


def add(parts):
    def body(*refs):
        refs[-1][...] = added(ref[...] for ref in refs[:-1])

    return pl.pallas_call(
        body,
        in_specs=[ON_CHIP] * len(parts),
        out_specs=ON_CHIP,
        out_shape=chip_shape(parts[0].shape),
        compiler_params=LIMITS,
        name="add",
    )(*[on_chip(part) for part in parts])


def rounds_of(size):
    bits = size.bit_length() - 1
    rounds = [(1,)] if bits % 2 else []
    for low in range(bits % 2, bits, 2):
        rounds.append((1 << low, 2 << low, 3 << low))
    return rounds


def sum_over(value, axis, size):
    parts = [value]
    for masks in rounds_of(size):
        value = parts[0] if len(parts) == 1 else add(parts)
        parts = [value]
        parts += [exchange(value, axis, size, mask) for mask in masks]
    return parts


def block_of(start, rows, most):
    return max(
        b for b in range(16, most + 1, 16) if b == 16 or not (rows % b or start % b)
    )


def rows_at(block):
    return pl.ds(pl.multiple_of(pl.program_id(0) * block, 16), block)


def peer_half(table, terms, token, chunk, places, width, chip):
    matrix, start, rows = chunk
    block = block_of(start, rows, STEP)

    def body(table_ref, *refs):
        out = refs[-1]
        at = rows_at(block) if chip else slice(None)
        for half in range(2):
            for p in range(places):
                out[half, p, at] = refs[half * places + p][...].astype(jnp.float32)

    def terms_spec(half, p):
        return pl.BlockSpec(
            (None, None, block, width),
            lambda i, t: (matrix, half, start // block + i, t[half, p] ^ 1),
        )

    specs = [terms_spec(half, p) for half in range(2) for p in range(places)]
    return pl.pallas_call(
        body,
        grid_spec=pltpu.PrefetchScalarGridSpec(
            num_scalar_prefetch=1,
            grid=(rows // block,),
            in_specs=[*specs, ANY],
            out_specs=ON_CHIP
            if chip
            else pl.BlockSpec((2, places, block, width), lambda i, t: (0, 0, i, 0)),
        ),
        out_shape=(chip_shape if chip else hbm_shape)((2, places, rows, width)),
        compiler_params=LIMITS,
        name="peer_half",
    )(table, *[terms] * len(specs), token)


def partial_sums(table, terms, from_peer, received, token, chunk, base, width, chip):
    matrix, start, rows = chunk
    block = block_of(start, rows, STEP)
    count = len(received)

    def body(table_ref, *refs):
        own, refs = refs[: 2 * base], refs[2 * base :]
        peer, others, outs = refs[0], refs[1 : 1 + 2 * count], refs[-2:]
        first, at = (base, rows_at(block)) if chip else (0, slice(None))
        for half in range(2):
            for p in range(base):
                total = own[half * base + p][...].astype(jnp.float32)
                total = total + peer[half, first + p, at]
                for k in range(count):
                    total = total + others[2 * k + half][first + p, at]
                outs[half][p, at] = total

    def terms_spec(half, p):
        return pl.BlockSpec(
            (None, None, block, width),
            lambda i, t: (matrix, half, start // block + i, t[half, base + p]),
        )

    specs = [terms_spec(half, p) for half in range(2) for p in range(base)]
    of_peer = pl.BlockSpec((2, base, block, width), lambda i, t: (0, 1, i, 0))
    shifted = pl.BlockSpec((base, block, width), lambda i, t: (1, i, 0))
    plain = pl.BlockSpec((base, block, width), lambda i, t: (0, i, 0))
    if chip:
        of_peer = shifted = plain = ON_CHIP
    shape = (chip_shape if chip else hbm_shape)((base, rows, width))
    put = on_chip if chip else in_hbm
    return pl.pallas_call(
        body,
        grid_spec=pltpu.PrefetchScalarGridSpec(
            num_scalar_prefetch=1,
            grid=(rows // block,),
            in_specs=[
                *specs,
                of_peer,
                *[shifted] * (2 * count),
                ANY,
            ],
            out_specs=[plain, plain],
        ),
        out_shape=[shape, shape],
        compiler_params=LIMITS,
        name="partial_sums",
    )(
        table, *[terms] * len(specs), put(from_peer),
        *[put(r) for pair in received for r in pair], token,
    )


def lane_groups(values, width):
    total = values[:, :LANES]
    for c in range(LANES, width, LANES):
        total = total + values[:, c : c + LANES]
    return total


def final_sums(table, terms, from_peer, received, totals, token, chunk, half_rows, width, chip):
    matrix, start, rows = chunk
    block = block_of(start, rows, STEP)
    steps = rows // block
    count = len(received)
    begin = totals is None

    def body(table_ref, own, peer, *refs):
        others = refs[: 2 * count]
        out, row_out, col_out, lanes = refs[-4:]
        i = pl.program_id(0)

        @pl.when(i == 0)
        def _():
            if begin:
                col_out[...] = jnp.zeros_like(col_out)

        for half in range(2):
            total = own[half].astype(jnp.float32)
            if chip:
                total = total + peer[half, 0, rows_at(block)]
            else:
                total = total + peer[half]
            for k in range(count):
                other = others[2 * k + half]
                total = total + (other[0, rows_at(block)] if chip else other[...])
            out[half, pl.ds(pl.multiple_of(start + i * block, 8), block), :] = total
            squares = total * total + tiny_square
            col_out[...] += jnp.sum(squares, axis=0, keepdims=True)
            lanes[half, pl.ds(pl.multiple_of(i * block, block), block), :] = lane_groups(
                squares, width
            )

        @pl.when(i == steps - 1)
        def _():
            for half in range(2):
                row_out[half : half + 1, start : start + rows] = jnp.sum(
                    lanes[half].T, axis=0, keepdims=True
                )

    of_peer = pl.BlockSpec((2, None, block, width), lambda i, t: (0, 0, i, 0))
    one = pl.BlockSpec((None, block, width), lambda i, t: (0, i, 0))
    if chip:
        of_peer = one = ON_CHIP
    put = on_chip if chip else in_hbm
    first = 3 + 2 * count
    return pl.pallas_call(
        body,
        grid_spec=pltpu.PrefetchScalarGridSpec(
            num_scalar_prefetch=1,
            grid=(steps,),
            in_specs=[
                pl.BlockSpec(
                    (None, 2, block, width),
                    lambda i, t: (matrix, 0, start // block + i, t[0, 0]),
                ),
                of_peer,
                *[one] * (2 * count),
                *([] if begin else [ON_CHIP] * 3),
                ANY,
            ],
            out_specs=[ON_CHIP] * 3,
            scratch_shapes=[pltpu.VMEM((2, rows, LANES), jnp.float32)],
        ),
        out_shape=[
            chip_shape((2, half_rows, width)),
            chip_shape((2, half_rows)),
            chip_shape((1, width)),
        ],
        input_output_aliases={} if begin else {first + k: k for k in range(3)},
        compiler_params=LIMITS,
        name="final_sums",
    )(
        table, terms, put(from_peer), *[put(r) for pair in received for r in pair],
        *([] if begin else [on_chip(v) for v in totals]), token,
    )


def down_rows(row):
    return jnp.broadcast_to(row, (LANES, LANES)).T


def over_rows(gradient, row_parts, columns, row_moment, new_rows, token, matrix, sizes):
    mats, rows, width, total_cols = sizes
    half_rows = rows // 2
    count = len(row_parts)
    begin = new_rows is None

    def body(g, *refs):
        parts, (col, old) = refs[:count], refs[count : count + 2]
        out, moments, message = refs[-3:]
        level = jnp.zeros((1, LANES), jnp.float32)
        squares = [jnp.zeros((8, LANES), jnp.float32)] * (width // LANES)
        for b in range(rows // LANES):
            half, first = b * LANES // half_rows, b * LANES % half_rows
            at = slice(first, first + LANES)
            total = added(part[half : half + 1, at] for part in parts)
            whole = slice(b * LANES, (b + 1) * LANES)
            moment = (
                second_decay * old[matrix : matrix + 1, whole]
                + (1.0 - second_decay) * total / total_cols
            )
            moments[matrix : matrix + 1, whole] = moment
            level = level + moment
            factor = down_rows(lax.rsqrt(moment))
            for k in range(width // LANES):
                lane = slice(k * LANES, (k + 1) * LANES)
                value = g[half, at, lane] * factor
                out[half, at, lane] = value
                squares[k] = squares[k] + jnp.sum(
                    (value * value).reshape(LANES // 8, 8, LANES), axis=0
                )
        message[0:1, :width] = col[...]
        message[0:1, width:] = level
        for k in range(width // LANES):
            message[1:2, k * LANES : (k + 1) * LANES] = jnp.sum(
                squares[k], axis=0, keepdims=True
            )
        message[1:2, width:] = jnp.zeros_like(level)

    return pl.pallas_call(
        body,
        in_specs=[ON_CHIP] * (3 + count + (0 if begin else 1)) + [ANY],
        out_specs=[ON_CHIP] * 3,
        out_shape=[
            chip_shape(gradient.shape),
            chip_shape((mats, rows)),
            chip_shape((2, width + LANES)),
        ],
        input_output_aliases={0: 0} if begin else {0: 0, 3 + count: 1},
        compiler_params=LIMITS,
        name="over_rows",
    )(
        *[on_chip(v) for v in (gradient, *row_parts, columns, row_moment)],
        *([] if begin else [on_chip(new_rows)]), token,
    )


def over_columns(messages, col_moment, sizes, total_rows):
    mats, _, width, _ = sizes
    count = len(messages[0])

    def body(*refs):
        old, new_cols, levels, lanes = refs[mats * count :]
        for matrix in range(mats):
            one = slice(matrix, matrix + 1)
            both = added(
                part[...] for part in refs[matrix * count : (matrix + 1) * count]
            )
            new = (
                second_decay * old[one, :]
                + (1.0 - second_decay) * both[0:1, :width] / total_rows
            )
            new_cols[one, :] = new
            lanes[one, :] = lane_groups(both[1:2, :width] / new, width)
            level = jnp.sum(both[0:1, width:], axis=1, keepdims=True) / total_rows
            levels[one, :] = jnp.broadcast_to(level, (1, LANES))

    return pl.pallas_call(
        body,
        in_specs=[ON_CHIP] * (mats * count + 1),
        out_specs=[ON_CHIP] * 3,
        out_shape=[
            chip_shape((mats, width)), chip_shape((mats, LANES)), chip_shape((mats, LANES)),
        ],
        compiler_params=LIMITS,
        name="over_columns",
    )(*[on_chip(v) for parts in messages for v in parts], on_chip(col_moment))


def scale(scaled, new_cols, levels, clip_parts, sizes, total_rows):
    mats, rows, width, total_cols = sizes
    half_rows = rows // 2
    pieces = 4
    piece = half_rows // pieces
    count = len(clip_parts)

    def body(*refs):
        c, level, *parts = refs[mats : mats + 2 + count]
        out, ready, sent = refs[-3:]

        def copy(matrix, half, k):
            at = pl.ds(half * half_rows + k * piece, piece)
            return pltpu.make_async_copy(
                ready.at[matrix, at], out.at[matrix, at], sent.at[matrix, half * pieces + k]
            )

        places = [
            (matrix, half, k)
            for matrix in range(mats) for half in range(2) for k in range(pieces)
        ]
        for matrix, half, k in places:
            one = slice(matrix, matrix + 1)
            if half == k == 0:
                row_level = level[one, :1]
                clip = jnp.sum(added(p[one, :] for p in parts), axis=1, keepdims=True)
                clip = jnp.sqrt(clip * row_level / (total_rows * total_cols))
                factor = lax.rsqrt(c[one, :]) * (jnp.sqrt(row_level) / jnp.maximum(1.0, clip))
            at = slice(k * piece, (k + 1) * piece)
            to = slice(half * half_rows + k * piece, half * half_rows + (k + 1) * piece)
            ready[matrix, to, :] = refs[matrix][half, at, :] * factor
            copy(matrix, half, k).start()
        for place in places:
            copy(*place).wait()

    return pl.pallas_call(
        body,
        in_specs=[ON_CHIP] * (mats + 2 + count),
        out_specs=ANY,
        out_shape=hbm_shape((mats, rows, width)),
        scratch_shapes=[
            pltpu.VMEM((mats, rows, width), jnp.float32),
            pltpu.SemaphoreType.DMA((mats, 2 * pieces)),
        ],
        compiler_params=LIMITS,
        name="scale",
    )(*[on_chip(v) for v in (*scaled, new_cols, levels, *clip_parts)])


def chunks_of(mats):
    chunks = []
    for matrix in range(mats):
        start = 0
        for size in LAST if matrix == mats - 1 else FIRST:
            chunks.append((matrix, start, size))
            start += size
    return chunks


def kernel_order(count, bits):
    order = [("peer", 0), ("peer", 1)]
    for t in range(-2, count + max(bits, 1)):
        step = [(f"sum{k}", t - k + 1) for k in range(1, bits)]
        step += [("final", t - max(bits - 1, 0))]
        step += [("sum0", t + 2)] if bits else []
        step += [("peer", t + 3)]
        order += [
            (stage, i) for stage, i in step if 0 <= i < count and (stage, i) not in order
        ]
    return order


def rounds_after(n_col):
    return 6 * len(rounds_of(n_col)) - 3


def on_device(n_row, n_col, grad_terms, row_moment, col_moment):
    _, mats, rows, all_width = grad_terms.shape
    width = all_width // n_col
    half_rows = rows // 2
    bits = n_col.bit_length() - 2
    places = 1 << bits
    total_rows, total_cols = rows * n_row, all_width
    sizes = (mats, rows, width, total_cols)

    me = lax.axis_index("col").astype(jnp.int32)
    terms = grad_terms.reshape(mats, 2, half_rows, all_width)
    orders = (tuple(range(bits)), tuple(reversed(range(bits))))

    def place_mask(order, place):
        return sum(1 << bit for k, bit in enumerate(order) if place >> (bits - 1 - k) & 1)

    masks = [[2 * place_mask(order, p) for p in range(places)] for order in orders]
    table = jnp.bitwise_xor(jnp.array(masks, jnp.int32), me)

    unit = half_rows // 16
    chunks = [(m, start * unit, size * unit) for m, start, size in chunks_of(mats)]
    last_of = {c[0]: i for i, c in enumerate(chunks)}

    from_peer, received = {}, {i: [] for i in range(len(chunks))}
    totals, row_parts, scaled = [None] * mats, [None] * mats, [None] * mats
    messages, new_rows = [None] * mats, None
    token = in_hbm(terms)

    def divide_rows(matrix):
        nonlocal new_rows, token
        gradient, _, columns = totals[matrix]
        scaled[matrix], new_rows, message = over_rows(
            gradient, row_parts[matrix], columns, row_moment, new_rows, token, matrix, sizes
        )
        token = on_chip(message)
        messages[matrix] = sum_over(message, "row", n_row)

    finished = []
    for stage, i in kernel_order(len(chunks), bits):
        for entry in finished:
            entry[1] -= 1
            if entry[1] == 0:
                divide_rows(entry[0])
        matrix = chunks[i][0]
        chip = i in ON_CHIP_CHUNKS or i - len(chunks) in ON_CHIP_CHUNKS
        put = on_chip if chip else in_hbm
        if stage == "peer":
            sent = peer_half(table, terms, token, chunks[i], places, width, chip)
        elif stage == "final":
            totals[matrix] = final_sums(
                table, terms, from_peer[i], received[i], totals[matrix], token,
                chunks[i], half_rows, width, chip,
            )
        else:
            k = int(stage[3:])
            sums = partial_sums(
                table, terms, from_peer[i], received[i], token, chunks[i],
                places >> (k + 1), width, chip,
            )
        if stage == "peer":
            token = put(sent)
            from_peer[i] = exchange(sent, "col", n_col, 1)
        elif stage == "final":
            token = on_chip(totals[matrix][2])
            if i == last_of[matrix]:
                row_parts[matrix] = sum_over(totals[matrix][1], "col", n_col)
                finished.append([matrix, rounds_after(n_col)])
        else:
            token = put(sums[0])
            received[i].append(
                [exchange(sums[half], "col", n_col, 2 << orders[half][k]) for half in range(2)]
            )
    for matrix in range(mats):
        if scaled[matrix] is None:
            divide_rows(matrix)

    new_cols, levels, lanes = over_columns(messages, col_moment, sizes, total_rows)
    clip_parts = sum_over(lanes, "col", n_col)
    update = scale(scaled, new_cols, levels, clip_parts, sizes, total_rows)
    return update, new_rows, new_cols


def solution(mesh):
    n_row, n_col = mesh.shape["row"], mesh.shape["col"]
    placed = (P("col", None, "row", None), P(None, "row"), P(None, "col"))

    def body(*args):
        return on_device(n_row, n_col, *args)

    return jax.shard_map(
        body,
        mesh=mesh,
        in_specs=placed,
        out_specs=(P(None, "row", "col"), P(None, "row"), P(None, "col")),
        check_vma=False,
    )
```

time: 554 us -> 536 us (0.968)
  Pallas kernels: 155 us -> 139 us
  starting transfers between devices: 49.8 us -> 59.7 us
  waiting for transfers between devices: 309 us -> 302 us
    ppermute x61 -> x68, starting transfers between devices: 49.8 us -> 59.7 us  [exchange(): return lax.ppermute(value, axis, [(i, i ^ mask) for i in range(size)])]
    pallas_call x20, Pallas kernels: 71.6 us -> 64.1 us  [partial_sums(): pl.pallas_call(body, grid_spec=pltpu.PrefetchScalarGridSpec(num_scalar_pr...]
    ppermute x61 -> x68, waiting for transfers between devices: 309 us -> 302 us  [exchange(): return lax.ppermute(value, axis, [(i, i ^ mask) for i in range(size)])]
    unnamed x181 -> x151, local copies, waits for them, and re-layouts: 35.9 us -> 30.4 us
  transfers between devices with their start and end apart: 61 -> 68, of which waited for: 34 -> 35; matrix products, arithmetic and copies ran while one was open for 0% -> 0% of each run, Pallas kernels for 12% -> 12%
where the time goes in v2:
time: 536 us; the launch traced here: 533 us
  waiting for transfers between devices  302 us (56%)
  Pallas kernels  139 us (26%)
  starting transfers between devices  59.7 us (11%)
  local copies, waits for them, and re-layouts  30.4 us (6%)
    ppermute x68, waiting for transfers between devices, exchange(): return lax.ppermute(value, axis, [(i, i ^ mask) for i in range(size)])  302 us
    pallas_call x20, Pallas kernels, partial_sums(): pl.pallas_call(body, grid_spec=pltpu.PrefetchScalarGridSpec(num_scalar_pr...  64.1 us
    ppermute x68, starting transfers between devices, exchange(): return lax.ppermute(value, axis, [(i, i ^ mask) for i in range(size)])  59.7 us
    pallas_call x10, Pallas kernels, peer_half(): pl.pallas_call(body, grid_spec=pltpu.PrefetchScalarGridSpec(num_scalar_pr...  39.4 us
    unnamed x151, local copies, waits for them, and re-layouts  30.4 us
    pallas_call x10, Pallas kernels, final_sums(): pl.pallas_call(body, grid_spec=pltpu.PrefetchScalarGridSpec(num_scalar_pr...  28.6 us
  transfers between devices with their start and end apart: 68, of which 35 were waited for; matrix products, arithmetic and copies ran while one was open for 0% of the time, Pallas kernels for 12%

profile of v2, /device:TPU:10, one launch (start us, length us, event | category | flops | bytes accessed | tf_op | source)
XLA Modules:
  0.0 533.2 jit_solution(95221927119953669)
XLA Ops:
  6.9 8.1 %collective-permute-done.1.refs_4_.refs_2_.peer = f32[2,4,32,1280]{3,2,1,0:T(8,128)S(1)} collective-permute-done((f32[2,4,32,1280]{3,2,1,0:T(8,128)S(1)}, f32[2,4,32,1280]{3,2,1,0:T(8,128)S(1)}, u32[]{:S(2)}, u32[]{:S(2)}) %collective-permute-start.1) | collective-permute-done | bytes 1310752 | tf_op jit(solution)/shard_map/ppermute | solution.py:37
  20.0 4.5 peer_half.12.refs_5_
  26.8 7.9 %collective-permute-done.4.refs_4_.refs_1_ = f32[2,32,1280]{2,1,0:T(8,128)S(1)} collective-permute-done((f32[2,32,1280]{2,1,0:T(8,128)S(1)}, f32[2,32,1280]{2,1,0:T(8,128)S(1)}, u32[]{:S(2)}, u32[]{:S(2)}) %collective-permute-start.4) | collective-permute-done | bytes 327712 | tf_op jit(solution)/shard_map/ppermute | solution.py:37
  39.9 4.0 partial_sums.23
  43.9 4.7 peer_half.13.refs_5_
  52.7 20.6 %collective-permute-done.9.refs_4_.refs_1_ = f32[2,96,1280]{2,1,0:T(8,128)S(1)} collective-permute-done((f32[2,96,1280]{2,1,0:T(8,128)S(1)}, f32[2,96,1280]{2,1,0:T(8,128)S(1)}, u32[]{:S(2)}, u32[]{:S(2)}) %collective-permute-start.9) | collective-permute-done | bytes 983072 | tf_op jit(solution)/shard_map/ppermute | solution.py:37
  80.6 4.0 partial_sums.25
  84.7 4.6 peer_half.14.refs_5_
  93.4 27.6 %collective-permute-done.14.refs_4_.refs_1_ = f32[2,128,1280]{2,1,0:T(8,128)S(1)} collective-permute-done((f32[2,128,1280]{2,1,0:T(8,128)S(1)}, f32[2,128,1280]{2,1,0:T(8,128)S(1)}, u32[]{:S(2)}, u32[]{:S(2)}) %collective-permute-start.14) | collective-permute-done | bytes 1310752 | tf_op jit(solution)/shard_map/ppermute | solution.py:37
  123.6 3.7 partial_sums.26
  127.3 4.9 collective-permute-done.12.refs_3_
  137.4 4.0 partial_sums.27
  141.4 4.8 peer_half.15.refs_5_
  150.3 27.6 %collective-permute-done.21.refs_4_.refs_1_ = f32[2,128,1280]{2,1,0:T(8,128)S(1)} collective-permute-done((f32[2,128,1280]{2,1,0:T(8,128)S(1)}, f32[2,128,1280]{2,1,0:T(8,128)S(1)}, u32[]{:S(2)}, u32[]{:S(2)}) %collective-permute-start.21) | collective-permute-done | bytes 1310752 | tf_op jit(solution)/shard_map/ppermute | solution.py:37
  183.6 8.1 %collective-permute-done.19.refs_3_ = f32[1,128,1280]{2,1,0:T(8,128)S(1)} collective-permute-done((f32[1,128,1280]{2,1,0:T(8,128)S(1)}, f32[1,128,1280]{2,1,0:T(8,128)S(1)}, u32[]{:S(2)}, u32[]{:S(2)}) %collective-permute-start.19) | collective-permute-done | bytes 655392 | tf_op jit(solution)/shard_map/ppermute | solution.py:37
  198.4 4.0 partial_sums.29
  202.5 4.8 peer_half.16.refs_5_
  211.4 27.6 %collective-permute-done.16.refs_4_.refs_1_ = f32[2,128,1280]{2,1,0:T(8,128)S(1)} collective-permute-done((f32[2,128,1280]{2,1,0:T(8,128)S(1)}, f32[2,128,1280]{2,1,0:T(8,128)S(1)}, u32[]{:S(2)}, u32[]{:S(2)}) %collective-permute-start.16) | collective-permute-done | bytes 1310752 | tf_op jit(solution)/shard_map/ppermute | solution.py:37
  245.1 8.7 %collective-permute-done.25.refs_3_ = f32[1,128,1280]{2,1,0:T(8,128)S(1)} collective-permute-done((f32[1,128,1280]{2,1,0:T(8,128)S(1)}, f32[1,128,1280]{2,1,0:T(8,128)S(1)}, u32[]{:S(2)}, u32[]{:S(2)}) %collective-permute-start.25) | collective-permute-done | bytes 655392 | tf_op jit(solution)/shard_map/ppermute | solution.py:37
  260.5 4.1 partial_sums.31
  264.6 4.8 peer_half.17.refs_5_
  273.5 27.6 %collective-permute-done.27.refs_4_.refs_1_ = f32[2,128,1280]{2,1,0:T(8,128)S(1)} collective-permute-done((f32[2,128,1280]{2,1,0:T(8,128)S(1)}, f32[2,128,1280]{2,1,0:T(8,128)S(1)}, u32[]{:S(2)}, u32[]{:S(2)}) %collective-permute-start.27) | collective-permute-done | bytes 1310752 | tf_op jit(solution)/shard_map/ppermute | solution.py:37
  306.7 8.1 %collective-permute-done.23.refs_3_ = f32[1,128,1280]{2,1,0:T(8,128)S(1)} collective-permute-done((f32[1,128,1280]{2,1,0:T(8,128)S(1)}, f32[1,128,1280]{2,1,0:T(8,128)S(1)}, u32[]{:S(2)}, u32[]{:S(2)}) %collective-permute-start.23) | collective-permute-done | bytes 655392 | tf_op jit(solution)/shard_map/ppermute | solution.py:37
  321.6 4.0 partial_sums.33
  325.6 3.9 peer_half.18.refs_5_
  333.6 27.6 %collective-permute-done.34.refs_4_.refs_1_ = f32[2,128,1280]{2,1,0:T(8,128)S(1)} collective-permute-done((f32[2,128,1280]{2,1,0:T(8,128)S(1)}, f32[2,128,1280]{2,1,0:T(8,128)S(1)}, u32[]{:S(2)}, u32[]{:S(2)}) %collective-permute-start.34) | collective-permute-done | bytes 1310752 | tf_op jit(solution)/shard_map/ppermute | solution.py:37
  367.3 8.7 %collective-permute-done.39.refs_3_ = f32[1,128,1280]{2,1,0:T(8,128)S(1)} collective-permute-done((f32[1,128,1280]{2,1,0:T(8,128)S(1)}, f32[1,128,1280]{2,1,0:T(8,128)S(1)}, u32[]{:S(2)}, u32[]{:S(2)}) %collective-permute-start.39) | collective-permute-done | bytes 655392 | tf_op jit(solution)/shard_map/ppermute | solution.py:37
  393.2 40.0 %collective-permute-done.37.refs_3_ = f32[1,128,1280]{2,1,0:T(8,128)S(1)} collective-permute-done((f32[1,128,1280]{2,1,0:T(8,128)S(1)}, f32[1,128,1280]{2,1,0:T(8,128)S(1)}, u32[]{:S(2)}, u32[]{:S(2)}) %collective-permute-start.37) | collective-permute-done | bytes 655392 | tf_op jit(solution)/shard_map/ppermute | solution.py:37
  456.7 6.3 %collective-permute-done.48.refs_3_.refs_0_ = f32[2,64,1280]{2,1,0:T(8,128)S(1)} collective-permute-done((f32[2,64,1280]{2,1,0:T(8,128)S(1)}, f32[2,64,1280]{2,1,0:T(8,128)S(1)}, u32[]{:S(2)}, u32[]{:S(2)}) %collective-permute-start.48) | collective-permute-done | bytes 655392 | tf_op jit(solution)/shard_map/ppermute | solution.py:37
  467.9 9.2 %collective-permute-done.47.refs_3_ = f32[1,128,1280]{2,1,0:T(8,128)S(1)} collective-permute-done((f32[1,128,1280]{2,1,0:T(8,128)S(1)}, f32[1,128,1280]{2,1,0:T(8,128)S(1)}, u32[]{:S(2)}, u32[]{:S(2)}) %collective-permute-start.47) | collective-permute-done | bytes 655392 | tf_op jit(solution)/shard_map/ppermute | solution.py:37
  481.7 9.4 %collective-permute-done.44.refs_3_.refs_0_ = f32[2,64,1280]{2,1,0:T(8,128)S(1)} collective-permute-done((f32[2,64,1280]{2,1,0:T(8,128)S(1)}, f32[2,64,1280]{2,1,0:T(8,128)S(1)}, u32[]{:S(2)}, u32[]{:S(2)}) %collective-permute-start.44) | collective-permute-done | bytes 655392 | tf_op jit(solution)/shard_map/ppermute | solution.py:37
  528.7 4.3 scale.1
  (303 shorter events, 189.3 us)
Async XLA Ops:
  89.3 45.8 %collective-permute-start.10 = (f32[2,4,128,1280]{3,2,1,0:T(8,128)}, f32[2,4,128,1280]{3,2,1,0:T(8,128)S(1)}, u32[]{:S(2)}, u32[]{:S(2)}) collective-permute-start(f32[2,4,128,1280]{3,2,1,0:T(8,128)} %peer_half.14.refs_5_), channel_id=1, source_target_pairs={{0,1},{1,0},{2,3},{3,2},{4,5},{5,4},{6,7},{7,6},{8,9},{9,8},{10,11... | collective-permute-start | bytes 15728648 | tf_op jit(solution)/shard_map/ppermute | solution.py:37
  89.3 31.7 %collective-permute-start.14 = (f32[2,128,1280]{2,1,0:T(8,128)S(1)}, f32[2,128,1280]{2,1,0:T(8,128)S(1)}, u32[]{:S(2)}, u32[]{:S(2)}) collective-permute-start(f32[2,128,1280]{2,1,0:T(8,128)S(1)} %copy-done.66), channel_id=1, source_target_pairs={{0,4},{1,5},{2,6},{3,7},{4,0},{5,1},{6,2},{7,3},{8,12},{9,13},{10,... | collective-permute-start | bytes 3932168 | tf_op jit(solution)/shard_map/ppermute | solution.py:37
  90.9 31.7 %collective-permute-start.13 = (f32[2,128,1280]{2,1,0:T(8,128)S(1)}, f32[2,128,1280]{2,1,0:T(8,128)S(1)}, u32[]{:S(2)}, u32[]{:S(2)}) collective-permute-start(f32[2,128,1280]{2,1,0:T(8,128)S(1)} %copy-done.39), channel_id=1, source_target_pairs={{0,2},{1,3},{2,0},{3,1},{4,6},{5,7},{6,4},{7,5},{8,10},{9,11},{10,... | collective-permute-start | bytes 3932168 | tf_op jit(solution)/shard_map/ppermute | solution.py:37
  91.4 40.8 %collective-permute-start.12 = (f32[1,96,1280]{2,1,0:T(8,128)S(1)}, f32[1,96,1280]{2,1,0:T(8,128)S(1)}, u32[]{:S(2)}, u32[]{:S(2)}) collective-permute-start(f32[1,96,1280]{2,1,0:T(8,128)S(1)} %get-tuple-element.92), channel_id=1, source_target_pairs={{0,2},{1,3},{2,0},{3,1},{4,6},{5,7},{6,4},{7,5},{8,10},{9,11},{10,... | collective-permute-start | bytes 1474568 | tf_op jit(solution)/shard_map/ppermute | solution.py:37
  92.9 39.3 %collective-permute-start.11 = (f32[1,96,1280]{2,1,0:T(8,128)S(1)}, f32[1,96,1280]{2,1,0:T(8,128)S(1)}, u32[]{:S(2)}, u32[]{:S(2)}) collective-permute-start(f32[1,96,1280]{2,1,0:T(8,128)S(1)} %get-tuple-element.89.refs_4_), channel_id=1, source_target_pairs={{0,4},{1,5},{2,6},{3,7},{4,0},{5,1},{6,2},{7,3},{8,12},{9,13},{10,... | collective-permute-start | bytes 1474568 | tf_op jit(solution)/shard_map/ppermute | solution.py:37
  146.2 49.8 %collective-permute-start.17 = (f32[2,4,128,1280]{3,2,1,0:T(8,128)}, f32[2,4,128,1280]{3,2,1,0:T(8,128)S(1)}, u32[]{:S(2)}, u32[]{:S(2)}) collective-permute-start(f32[2,4,128,1280]{3,2,1,0:T(8,128)} %peer_half.15.refs_5_), channel_id=1, source_target_pairs={{0,1},{1,0},{2,3},{3,2},{4,5},{5,4},{6,7},{7,6},{8,9},{9,8},{10,11... | collective-permute-start | bytes 15728648 | tf_op jit(solution)/shard_map/ppermute | solution.py:37
  146.2 31.7 %collective-permute-start.21 = (f32[2,128,1280]{2,1,0:T(8,128)S(1)}, f32[2,128,1280]{2,1,0:T(8,128)S(1)}, u32[]{:S(2)}, u32[]{:S(2)}) collective-permute-start(f32[2,128,1280]{2,1,0:T(8,128)S(1)} %copy-done.62), channel_id=1, source_target_pairs={{0,4},{1,5},{2,6},{3,7},{4,0},{5,1},{6,2},{7,3},{8,12},{9,13},{10,... | collective-permute-start | bytes 3932168 | tf_op jit(solution)/shard_map/ppermute | solution.py:37
  146.8 31.7 %collective-permute-start.20 = (f32[2,128,1280]{2,1,0:T(8,128)S(1)}, f32[2,128,1280]{2,1,0:T(8,128)S(1)}, u32[]{:S(2)}, u32[]{:S(2)}) collective-permute-start(f32[2,128,1280]{2,1,0:T(8,128)S(1)} %copy-done.35), channel_id=1, source_target_pairs={{0,2},{1,3},{2,0},{3,1},{4,6},{5,7},{6,4},{7,5},{8,10},{9,11},{10,... | collective-permute-start | bytes 3932168 | tf_op jit(solution)/shard_map/ppermute | solution.py:37
  147.3 44.3 %collective-permute-start.19 = (f32[1,128,1280]{2,1,0:T(8,128)S(1)}, f32[1,128,1280]{2,1,0:T(8,128)S(1)}, u32[]{:S(2)}, u32[]{:S(2)}) collective-permute-start(f32[1,128,1280]{2,1,0:T(8,128)S(1)} %copy-done.69), channel_id=1, source_target_pairs={{0,2},{1,3},{2,0},{3,1},{4,6},{5,7},{6,4},{7,5},{8,10},{9,11},{10,... | collective-permute-start | bytes 1966088 | tf_op jit(solution)/shard_map/ppermute | solution.py:37
  148.8 42.9 %collective-permute-start.18 = (f32[1,128,1280]{2,1,0:T(8,128)S(1)}, f32[1,128,1280]{2,1,0:T(8,128)S(1)}, u32[]{:S(2)}, u32[]{:S(2)}) collective-permute-start(f32[1,128,1280]{2,1,0:T(8,128)S(1)} %copy-done.53), channel_id=1, source_target_pairs={{0,4},{1,5},{2,6},{3,7},{4,0},{5,1},{6,2},{7,3},{8,12},{9,13},{10,... | collective-permute-start | bytes 1966088 | tf_op jit(solution)/shard_map/ppermute | solution.py:37
  207.2 50.9 %collective-permute-start.28 = (f32[2,4,128,1280]{3,2,1,0:T(8,128)}, f32[2,4,128,1280]{3,2,1,0:T(8,128)S(1)}, u32[]{:S(2)}, u32[]{:S(2)}) collective-permute-start(f32[2,4,128,1280]{3,2,1,0:T(8,128)} %peer_half.16.refs_5_), channel_id=1, source_target_pairs={{0,1},{1,0},{2,3},{3,2},{4,5},{5,4},{6,7},{7,6},{8,9},{9,8},{10,11... | collective-permute-start | bytes 15728648 | tf_op jit(solution)/shard_map/ppermute | solution.py:37
  207.3 31.7 %collective-permute-start.16 = (f32[2,128,1280]{2,1,0:T(8,128)S(1)}, f32[2,128,1280]{2,1,0:T(8,128)S(1)}, u32[]{:S(2)}, u32[]{:S(2)}) collective-permute-start(f32[2,128,1280]{2,1,0:T(8,128)S(1)} %copy-done.63), channel_id=1, source_target_pairs={{0,4},{1,5},{2,6},{3,7},{4,0},{5,1},{6,2},{7,3},{8,12},{9,13},{10,... | collective-permute-start | bytes 3932168 | tf_op jit(solution)/shard_map/ppermute | solution.py:37
  208.8 31.7 %collective-permute-start.15 = (f32[2,128,1280]{2,1,0:T(8,128)S(1)}, f32[2,128,1280]{2,1,0:T(8,128)S(1)}, u32[]{:S(2)}, u32[]{:S(2)}) collective-permute-start(f32[2,128,1280]{2,1,0:T(8,128)S(1)} %copy-done.36), channel_id=1, source_target_pairs={{0,2},{1,3},{2,0},{3,1},{4,6},{5,7},{6,4},{7,5},{8,10},{9,11},{10,... | collective-permute-start | bytes 3932168 | tf_op jit(solution)/shard_map/ppermute | solution.py:37
  209.4 44.3 %collective-permute-start.25 = (f32[1,128,1280]{2,1,0:T(8,128)S(1)}, f32[1,128,1280]{2,1,0:T(8,128)S(1)}, u32[]{:S(2)}, u32[]{:S(2)}) collective-permute-start(f32[1,128,1280]{2,1,0:T(8,128)S(1)} %copy-done.70), channel_id=1, source_target_pairs={{0,2},{1,3},{2,0},{3,1},{4,6},{5,7},{6,4},{7,5},{8,10},{9,11},{10,... | collective-permute-start | bytes 1966088 | tf_op jit(solution)/shard_map/ppermute | solution.py:37
  210.9 42.9 %collective-permute-start.24 = (f32[1,128,1280]{2,1,0:T(8,128)S(1)}, f32[1,128,1280]{2,1,0:T(8,128)S(1)}, u32[]{:S(2)}, u32[]{:S(2)}) collective-permute-start(f32[1,128,1280]{2,1,0:T(8,128)S(1)} %copy-done.42), channel_id=1, source_target_pairs={{0,4},{1,5},{2,6},{3,7},{4,0},{5,1},{6,2},{7,3},{8,12},{9,13},{10,... | collective-permute-start | bytes 1966088 | tf_op jit(solution)/shard_map/ppermute | solution.py:37
  269.3 50.0 %collective-permute-start.35 = (f32[2,4,128,1280]{3,2,1,0:T(8,128)}, f32[2,4,128,1280]{3,2,1,0:T(8,128)S(1)}, u32[]{:S(2)}, u32[]{:S(2)}) collective-permute-start(f32[2,4,128,1280]{3,2,1,0:T(8,128)} %peer_half.17.refs_5_), channel_id=1, source_target_pairs={{0,1},{1,0},{2,3},{3,2},{4,5},{5,4},{6,7},{7,6},{8,9},{9,8},{10,11... | collective-permute-start | bytes 15728648 | tf_op jit(solution)/shard_map/ppermute | solution.py:37
  269.4 31.7 %collective-permute-start.27 = (f32[2,128,1280]{2,1,0:T(8,128)S(1)}, f32[2,128,1280]{2,1,0:T(8,128)S(1)}, u32[]{:S(2)}, u32[]{:S(2)}) collective-permute-start(f32[2,128,1280]{2,1,0:T(8,128)S(1)} %copy-done.64), channel_id=1, source_target_pairs={{0,4},{1,5},{2,6},{3,7},{4,0},{5,1},{6,2},{7,3},{8,12},{9,13},{10,... | collective-permute-start | bytes 3932168 | tf_op jit(solution)/shard_map/ppermute | solution.py:37
  269.9 31.7 %collective-permute-start.26 = (f32[2,128,1280]{2,1,0:T(8,128)S(1)}, f32[2,128,1280]{2,1,0:T(8,128)S(1)}, u32[]{:S(2)}, u32[]{:S(2)}) collective-permute-start(f32[2,128,1280]{2,1,0:T(8,128)S(1)} %copy-done.37), channel_id=1, source_target_pairs={{0,2},{1,3},{2,0},{3,1},{4,6},{5,7},{6,4},{7,5},{8,10},{9,11},{10,... | collective-permute-start | bytes 3932168 | tf_op jit(solution)/shard_map/ppermute | solution.py:37
  270.5 44.3 %collective-permute-start.23 = (f32[1,128,1280]{2,1,0:T(8,128)S(1)}, f32[1,128,1280]{2,1,0:T(8,128)S(1)}, u32[]{:S(2)}, u32[]{:S(2)}) collective-permute-start(f32[1,128,1280]{2,1,0:T(8,128)S(1)} %copy-done.71), channel_id=1, source_target_pairs={{0,2},{1,3},{2,0},{3,1},{4,6},{5,7},{6,4},{7,5},{8,10},{9,11},{10,... | collective-permute-start | bytes 1966088 | tf_op jit(solution)/shard_map/ppermute | solution.py:37
  272.0 42.9 %collective-permute-start.22 = (f32[1,128,1280]{2,1,0:T(8,128)S(1)}, f32[1,128,1280]{2,1,0:T(8,128)S(1)}, u32[]{:S(2)}, u32[]{:S(2)}) collective-permute-start(f32[1,128,1280]{2,1,0:T(8,128)S(1)} %copy-done.43), channel_id=1, source_target_pairs={{0,4},{1,5},{2,6},{3,7},{4,0},{5,1},{6,2},{7,3},{8,12},{9,13},{10,... | collective-permute-start | bytes 1966088 | tf_op jit(solution)/shard_map/ppermute | solution.py:37
  329.5 51.0 %collective-permute-start.42 = (f32[2,4,64,1280]{3,2,1,0:T(8,128)}, f32[2,4,64,1280]{3,2,1,0:T(8,128)S(1)}, u32[]{:S(2)}, u32[]{:S(2)}) collective-permute-start(f32[2,4,64,1280]{3,2,1,0:T(8,128)} %peer_half.18.refs_5_), channel_id=1, source_target_pairs={{0,1},{1,0},{2,3},{3,2},{4,5},{5,4},{6,7},{7,6},{8,9},{9,8},{10,11... | collective-permute-start | bytes 7864328 | tf_op jit(solution)/shard_map/ppermute | solution.py:37
  329.5 31.7 %collective-permute-start.34 = (f32[2,128,1280]{2,1,0:T(8,128)S(1)}, f32[2,128,1280]{2,1,0:T(8,128)S(1)}, u32[]{:S(2)}, u32[]{:S(2)}) collective-permute-start(f32[2,128,1280]{2,1,0:T(8,128)S(1)} %copy-done.65), channel_id=1, source_target_pairs={{0,4},{1,5},{2,6},{3,7},{4,0},{5,1},{6,2},{7,3},{8,12},{9,13},{10,... | collective-permute-start | bytes 3932168 | tf_op jit(solution)/shard_map/ppermute | solution.py:37
  331.1 31.6 %collective-permute-start.33 = (f32[2,128,1280]{2,1,0:T(8,128)S(1)}, f32[2,128,1280]{2,1,0:T(8,128)S(1)}, u32[]{:S(2)}, u32[]{:S(2)}) collective-permute-start(f32[2,128,1280]{2,1,0:T(8,128)S(1)} %copy-done.38), channel_id=1, source_target_pairs={{0,2},{1,3},{2,0},{3,1},{4,6},{5,7},{6,4},{7,5},{8,10},{9,11},{10,... | collective-permute-start | bytes 3932168 | tf_op jit(solution)/shard_map/ppermute | solution.py:37
  331.6 44.3 %collective-permute-start.39 = (f32[1,128,1280]{2,1,0:T(8,128)S(1)}, f32[1,128,1280]{2,1,0:T(8,128)S(1)}, u32[]{:S(2)}, u32[]{:S(2)}) collective-permute-start(f32[1,128,1280]{2,1,0:T(8,128)S(1)} %copy-done.72), channel_id=1, source_target_pairs={{0,2},{1,3},{2,0},{3,1},{4,6},{5,7},{6,4},{7,5},{8,10},{9,11},{10,... | collective-permute-start | bytes 1966088 | tf_op jit(solution)/shard_map/ppermute | solution.py:37
  333.1 42.9 %collective-permute-start.38 = (f32[1,128,1280]{2,1,0:T(8,128)S(1)}, f32[1,128,1280]{2,1,0:T(8,128)S(1)}, u32[]{:S(2)}, u32[]{:S(2)}) collective-permute-start(f32[1,128,1280]{2,1,0:T(8,128)S(1)} %copy-done.44), channel_id=1, source_target_pairs={{0,4},{1,5},{2,6},{3,7},{4,0},{5,1},{6,2},{7,3},{8,12},{9,13},{10,... | collective-permute-start | bytes 1966088 | tf_op jit(solution)/shard_map/ppermute | solution.py:37
  387.7 65.1 %collective-permute-start.43 = (f32[2,4,64,1280]{3,2,1,0:T(8,128)S(1)}, f32[2,4,64,1280]{3,2,1,0:T(8,128)S(1)}, u32[]{:S(2)}, u32[]{:S(2)}) collective-permute-start(f32[2,4,64,1280]{3,2,1,0:T(8,128)S(1)} %peer_half.19.refs_5_), channel_id=1, source_target_pairs={{0,1},{1,0},{2,3},{3,2},{4,5},{5,4},{6,7},{7,6},{8,9},{9,8},{10,11... | collective-permute-start | bytes 7864328 | tf_op jit(solution)/shard_map/ppermute | solution.py:37
  387.8 47.6 %collective-permute-start.41 = (f32[2,128,1280]{2,1,0:T(8,128)S(1)}, f32[2,128,1280]{2,1,0:T(8,128)S(1)}, u32[]{:S(2)}, u32[]{:S(2)}) collective-permute-start(f32[2,128,1280]{2,1,0:T(8,128)S(1)} %copy-done.61), channel_id=1, source_target_pairs={{0,4},{1,5},{2,6},{3,7},{4,0},{5,1},{6,2},{7,3},{8,12},{9,13},{10,... | collective-permute-start | bytes 3932168 | tf_op jit(solution)/shard_map/ppermute | solution.py:37
  388.4 48.5 %collective-permute-start.40 = (f32[2,128,1280]{2,1,0:T(8,128)S(1)}, f32[2,128,1280]{2,1,0:T(8,128)S(1)}, u32[]{:S(2)}, u32[]{:S(2)}) collective-permute-start(f32[2,128,1280]{2,1,0:T(8,128)S(1)} %copy-done.34), channel_id=1, source_target_pairs={{0,2},{1,3},{2,0},{3,1},{4,6},{5,7},{6,4},{7,5},{8,10},{9,11},{10,... | collective-permute-start | bytes 3932168 | tf_op jit(solution)/shard_map/ppermute | solution.py:37
  389.1 44.2 %collective-permute-start.37 = (f32[1,128,1280]{2,1,0:T(8,128)S(1)}, f32[1,128,1280]{2,1,0:T(8,128)S(1)}, u32[]{:S(2)}, u32[]{:S(2)}) collective-permute-start(f32[1,128,1280]{2,1,0:T(8,128)S(1)} %copy-done.73), channel_id=1, source_target_pairs={{0,2},{1,3},{2,0},{3,1},{4,6},{5,7},{6,4},{7,5},{8,10},{9,11},{10,... | collective-permute-start | bytes 1966088 | tf_op jit(solution)/shard_map/ppermute | solution.py:37
  392.7 42.1 %collective-permute-start.36 = (f32[1,128,1280]{2,1,0:T(8,128)S(1)}, f32[1,128,1280]{2,1,0:T(8,128)S(1)}, u32[]{:S(2)}, u32[]{:S(2)}) collective-permute-start(f32[1,128,1280]{2,1,0:T(8,128)S(1)} %copy-done.54), channel_id=1, source_target_pairs={{0,4},{1,5},{2,6},{3,7},{4,0},{5,1},{6,2},{7,3},{8,12},{9,13},{10,... | collective-permute-start | bytes 1966088 | tf_op jit(solution)/shard_map/ppermute | solution.py:37
  455.4 35.8 %collective-permute-start.44 = (f32[2,64,1280]{2,1,0:T(8,128)S(1)}, f32[2,64,1280]{2,1,0:T(8,128)S(1)}, u32[]{:S(2)}, u32[]{:S(2)}) collective-permute-start(f32[2,64,1280]{2,1,0:T(8,128)S(1)} %get-tuple-element.135.refs_5_), channel_id=1, source_target_pairs={{0,2},{1,3},{2,0},{3,1},{4,6},{5,7},{6,4},{7,5},{8,10},{9,11},{10,... | collective-permute-start | bytes 1966088 | tf_op jit(solution)/shard_map/ppermute | solution.py:37
  466.8 31.3 %collective-permute-start.53 = (f32[1,64,1280]{2,1,0:T(8,128)}, f32[1,64,1280]{2,1,0:T(8,128)S(1)}, u32[]{:S(2)}, u32[]{:S(2)}) collective-permute-start(f32[1,64,1280]{2,1,0:T(8,128)} %get-tuple-element.145), channel_id=1, source_target_pairs={{0,2},{1,3},{2,0},{3,1},{4,6},{5,7},{6,4},{7,5},{8,10},{9,11},{10,... | collective-permute-start | bytes 983048 | tf_op jit(solution)/shard_map/ppermute | solution.py:37
  (110 other events, 897.7 us)

commit v3 on v2

--- a/solution.py
+++ b/solution.py
@@ -321,85 +321,86 @@
     )
 
 
-def over_columns(messages, col_moment, sizes, total_rows):
+def over_columns(parts, col_moment, others, matrix, sizes, total_rows):
     mats, _, width, _ = sizes
-    count = len(messages[0])
+    count = len(parts)
 
     def body(*refs):
-        old, new_cols, levels, lanes = refs[mats * count :]
-        for matrix in range(mats):
-            one = slice(matrix, matrix + 1)
-            both = added(
-                part[...] for part in refs[matrix * count : (matrix + 1) * count]
-            )
-            new = (
-                second_decay * old[one, :]
-                + (1.0 - second_decay) * both[0:1, :width] / total_rows
-            )
-            new_cols[one, :] = new
-            lanes[one, :] = lane_groups(both[1:2, :width] / new, width)
-            level = jnp.sum(both[0:1, width:], axis=1, keepdims=True) / total_rows
-            levels[one, :] = jnp.broadcast_to(level, (1, LANES))
-
-    return pl.pallas_call(
-        body,
-        in_specs=[ON_CHIP] * (mats * count + 1),
-        out_specs=[ON_CHIP] * 3,
-        out_shape=[
-            chip_shape((mats, width)), chip_shape((mats, LANES)), chip_shape((mats, LANES)),
-        ],
+        old = refs[count]
+        new_cols, levels, lanes = refs[count + 1 + len(others) :][:3]
+        both = added(part[...] for part in refs[:count])
+        new = (
+            second_decay * old[matrix : matrix + 1, :]
+            + (1.0 - second_decay) * both[0:1, :width] / total_rows
+        )
+        new_cols[...] = new
+        lanes[...] = lane_groups(both[1:2, :width] / new, width)
+        level = jnp.sum(both[0:1, width:], axis=1, keepdims=True) / total_rows
+        levels[...] = jnp.broadcast_to(level, (1, LANES))
+        if others:
+            for k, other in enumerate(refs[count + 1 :][: len(others)]):
+                refs[-1][k : k + 1, :] = other[...]
+            refs[-1][matrix : matrix + 1, :] = new
+
+    outs = [chip_shape((1, width)), chip_shape((1, LANES)), chip_shape((1, LANES))]
+    outs += [chip_shape((mats, width))] if others else []
+    return pl.pallas_call(
+        body,
+        in_specs=[ON_CHIP] * (count + 1 + len(others)),
+        out_specs=[ON_CHIP] * len(outs),
+        out_shape=outs,
         compiler_params=LIMITS,
         name="over_columns",
-    )(*[on_chip(v) for parts in messages for v in parts], on_chip(col_moment))
-
-
-def scale(scaled, new_cols, levels, clip_parts, sizes, total_rows):
+    )(*[on_chip(v) for v in (*parts, col_moment, *others)])
+
+
+def scale(scaled, new_cols, levels, clip_parts, output, matrix, sizes, total_rows):
     mats, rows, width, total_cols = sizes
     half_rows = rows // 2
     pieces = 4
     piece = half_rows // pieces
     count = len(clip_parts)
-
-    def body(*refs):
-        c, level, *parts = refs[mats : mats + 2 + count]
+    begin = output is None
+
+    def body(g, c, level, *refs):
+        parts = refs[:count]
         out, ready, sent = refs[-3:]
-
-        def copy(matrix, half, k):
+        row_level = level[:, :1]
+        clip = jnp.sum(added(p[...] for p in parts), axis=1, keepdims=True)
+        clip = jnp.sqrt(clip * row_level / (total_rows * total_cols))
+        factor = lax.rsqrt(c[...]) * (jnp.sqrt(row_level) / jnp.maximum(1.0, clip))
+
+        def copy(half, k):
             at = pl.ds(half * half_rows + k * piece, piece)
             return pltpu.make_async_copy(
-                ready.at[matrix, at], out.at[matrix, at], sent.at[matrix, half * pieces + k]
-            )
-
-        places = [
-            (matrix, half, k)
-            for matrix in range(mats) for half in range(2) for k in range(pieces)
-        ]
-        for matrix, half, k in places:
-            one = slice(matrix, matrix + 1)
-            if half == k == 0:
-                row_level = level[one, :1]
-                clip = jnp.sum(added(p[one, :] for p in parts), axis=1, keepdims=True)
-                clip = jnp.sqrt(clip * row_level / (total_rows * total_cols))
-                factor = lax.rsqrt(c[one, :]) * (jnp.sqrt(row_level) / jnp.maximum(1.0, clip))
+                ready.at[at], out.at[matrix, at], sent.at[half * pieces + k]
+            )
+
+        places = [(half, k) for half in range(2) for k in range(pieces)]
+        for half, k in places:
             at = slice(k * piece, (k + 1) * piece)
             to = slice(half * half_rows + k * piece, half * half_rows + (k + 1) * piece)
-            ready[matrix, to, :] = refs[matrix][half, at, :] * factor
-            copy(matrix, half, k).start()
+            ready[to, :] = g[half, at, :] * factor
+            copy(half, k).start()
         for place in places:
             copy(*place).wait()
 
     return pl.pallas_call(
         body,
-        in_specs=[ON_CHIP] * (mats + 2 + count),
+        in_specs=[ON_CHIP] * (3 + count) + ([] if begin else [ANY]),
         out_specs=ANY,
         out_shape=hbm_shape((mats, rows, width)),
+        input_output_aliases={} if begin else {3 + count: 0},
         scratch_shapes=[
-            pltpu.VMEM((mats, rows, width), jnp.float32),
-            pltpu.SemaphoreType.DMA((mats, 2 * pieces)),
+            pltpu.VMEM((rows, width), jnp.float32),
+            pltpu.SemaphoreType.DMA((2 * pieces,)),
         ],
         compiler_params=LIMITS,
         name="scale",
-    )(*[on_chip(v) for v in (*scaled, new_cols, levels, *clip_parts)])
+    )(
+        *[on_chip(v) for v in (scaled, new_cols, levels, *clip_parts)],
+        *([] if begin else [in_hbm(output)]),
+    )
 
 
 def chunks_of(mats):
@@ -426,7 +427,7 @@
 
 
 def rounds_after(n_col):
-    return 6 * len(rounds_of(n_col)) - 3
+    return 5 * len(rounds_of(n_col)) - 2
 
 
 def on_device(n_row, n_col, grad_terms, row_moment, col_moment):
@@ -454,17 +455,24 @@
 
     from_peer, received = {}, {i: [] for i in range(len(chunks))}
     totals, row_parts, scaled = [None] * mats, [None] * mats, [None] * mats
-    messages, new_rows = [None] * mats, None
+    moved, new_rows, new_cols = [], None, None
     token = in_hbm(terms)
 
     def divide_rows(matrix):
-        nonlocal new_rows, token
+        nonlocal new_rows, new_cols, token
         gradient, _, columns = totals[matrix]
         scaled[matrix], new_rows, message = over_rows(
             gradient, row_parts[matrix], columns, row_moment, new_rows, token, matrix, sizes
         )
         token = on_chip(message)
-        messages[matrix] = sum_over(message, "row", n_row)
+        parts = sum_over(message, "row", n_row)
+        others = [c for c, *_ in moved] if matrix == mats - 1 else []
+        c, levels, lanes, *all_cols = over_columns(
+            parts, col_moment, others, matrix, sizes, total_rows
+        )
+        new_cols = all_cols[0] if all_cols else c
+        clip_parts = sum_over(lanes, "col", n_col)
+        moved.append((c, levels, clip_parts))
 
     finished = []
     for stage, i in kernel_order(len(chunks), bits):
@@ -505,9 +513,11 @@
         if scaled[matrix] is None:
             divide_rows(matrix)
 
-    new_cols, levels, lanes = over_columns(messages, col_moment, sizes, total_rows)
-    clip_parts = sum_over(lanes, "col", n_col)
-    update = scale(scaled, new_cols, levels, clip_parts, sizes, total_rows)
+    update = None
+    for matrix in range(mats):
+        update = scale(
+            scaled[matrix], *moved[matrix], update, matrix, sizes, total_rows
+        )
     return update, new_rows, new_cols
 
 

time: 536 us -> 529 us (0.987)
  waiting for transfers between devices: 302 us -> 290 us
    ppermute x68 -> x72, waiting for transfers between devices: 302 us -> 290 us  [exchange(): return lax.ppermute(value, axis, [(i, i ^ mask) for i in range(size)])]
    ppermute x68 -> x72, starting transfers between devices: 59.7 us -> 62.2 us  [exchange(): return lax.ppermute(value, axis, [(i, i ^ mask) for i in range(size)])]
    unnamed x151 -> x153, local copies, waits for them, and re-layouts: 30.4 us -> 30.4 us
  transfers between devices with their start and end apart: 68 -> 72, of which waited for: 35 -> 33; matrix products, arithmetic and copies ran while one was open for 0% -> 0% of each run, Pallas kernels for 12% -> 13%
where the time goes in v3:
time: 529 us; the launch traced here: 525 us
  waiting for transfers between devices  290 us (55%)
  Pallas kernels  140 us (26%)
  starting transfers between devices  62.2 us (12%)
  local copies, waits for them, and re-layouts  30.4 us (6%)
    ppermute x72, waiting for transfers between devices, exchange(): return lax.ppermute(value, axis, [(i, i ^ mask) for i in range(size)])  290 us
    pallas_call x20, Pallas kernels, partial_sums(): pl.pallas_call(body, grid_spec=pltpu.PrefetchScalarGridSpec(num_scalar_pr...  64.2 us
    ppermute x72, starting transfers between devices, exchange(): return lax.ppermute(value, axis, [(i, i ^ mask) for i in range(size)])  62.2 us
    pallas_call x10, Pallas kernels, peer_half(): pl.pallas_call(body, grid_spec=pltpu.PrefetchScalarGridSpec(num_scalar_pr...  39.3 us
    unnamed x153, local copies, waits for them, and re-layouts  30.4 us
    pallas_call x10, Pallas kernels, final_sums(): pl.pallas_call(body, grid_spec=pltpu.PrefetchScalarGridSpec(num_scalar_pr...  28.7 us
  transfers between devices with their start and end apart: 72, of which 33 were waited for; matrix products, arithmetic and copies ran while one was open for 0% of the time, Pallas kernels for 13%

profile of v3, /device:TPU:10, one launch (start us, length us, event | category | flops | bytes accessed | tf_op | source)
XLA Modules:
  0.0 525.5 jit_solution(7631019110449970220)
XLA Ops:
  6.9 8.1 %collective-permute-done.1.refs_4_.refs_2_.peer = f32[2,4,32,1280]{3,2,1,0:T(8,128)S(1)} collective-permute-done((f32[2,4,32,1280]{3,2,1,0:T(8,128)S(1)}, f32[2,4,32,1280]{3,2,1,0:T(8,128)S(1)}, u32[]{:S(2)}, u32[]{:S(2)}) %collective-permute-start.1) | collective-permute-done | bytes 1310752 | tf_op jit(solution)/shard_map/ppermute | solution.py:37
  20.0 4.5 peer_half.12.refs_5_
  26.8 7.9 %collective-permute-done.4.refs_4_.refs_1_ = f32[2,32,1280]{2,1,0:T(8,128)S(1)} collective-permute-done((f32[2,32,1280]{2,1,0:T(8,128)S(1)}, f32[2,32,1280]{2,1,0:T(8,128)S(1)}, u32[]{:S(2)}, u32[]{:S(2)}) %collective-permute-start.4) | collective-permute-done | bytes 327712 | tf_op jit(solution)/shard_map/ppermute | solution.py:37
  39.9 4.0 partial_sums.23
  43.9 4.7 peer_half.13.refs_5_
  52.7 20.6 %collective-permute-done.9.refs_4_.refs_1_ = f32[2,96,1280]{2,1,0:T(8,128)S(1)} collective-permute-done((f32[2,96,1280]{2,1,0:T(8,128)S(1)}, f32[2,96,1280]{2,1,0:T(8,128)S(1)}, u32[]{:S(2)}, u32[]{:S(2)}) %collective-permute-start.9) | collective-permute-done | bytes 983072 | tf_op jit(solution)/shard_map/ppermute | solution.py:37
  80.5 4.1 partial_sums.25
  84.6 4.7 peer_half.14.refs_5_
  93.4 27.6 %collective-permute-done.14.refs_4_.refs_1_ = f32[2,128,1280]{2,1,0:T(8,128)S(1)} collective-permute-done((f32[2,128,1280]{2,1,0:T(8,128)S(1)}, f32[2,128,1280]{2,1,0:T(8,128)S(1)}, u32[]{:S(2)}, u32[]{:S(2)}) %collective-permute-start.14) | collective-permute-done | bytes 1310752 | tf_op jit(solution)/shard_map/ppermute | solution.py:37
  127.3 4.9 collective-permute-done.12.refs_3_
  137.5 4.1 partial_sums.27
  141.5 4.7 peer_half.15.refs_5_
  150.4 27.6 %collective-permute-done.19.refs_4_.refs_1_ = f32[2,128,1280]{2,1,0:T(8,128)S(1)} collective-permute-done((f32[2,128,1280]{2,1,0:T(8,128)S(1)}, f32[2,128,1280]{2,1,0:T(8,128)S(1)}, u32[]{:S(2)}, u32[]{:S(2)}) %collective-permute-start.19) | collective-permute-done | bytes 1310752 | tf_op jit(solution)/shard_map/ppermute | solution.py:37
  183.6 8.1 %collective-permute-done.17.refs_3_ = f32[1,128,1280]{2,1,0:T(8,128)S(1)} collective-permute-done((f32[1,128,1280]{2,1,0:T(8,128)S(1)}, f32[1,128,1280]{2,1,0:T(8,128)S(1)}, u32[]{:S(2)}, u32[]{:S(2)}) %collective-permute-start.17) | collective-permute-done | bytes 655392 | tf_op jit(solution)/shard_map/ppermute | solution.py:37
  198.5 4.1 partial_sums.29
  202.6 4.7 peer_half.16.refs_5_
  211.4 27.6 %collective-permute-done.24.refs_4_.refs_1_ = f32[2,128,1280]{2,1,0:T(8,128)S(1)} collective-permute-done((f32[2,128,1280]{2,1,0:T(8,128)S(1)}, f32[2,128,1280]{2,1,0:T(8,128)S(1)}, u32[]{:S(2)}, u32[]{:S(2)}) %collective-permute-start.24) | collective-permute-done | bytes 1310752 | tf_op jit(solution)/shard_map/ppermute | solution.py:37
  245.1 8.7 %collective-permute-done.22.refs_3_ = f32[1,128,1280]{2,1,0:T(8,128)S(1)} collective-permute-done((f32[1,128,1280]{2,1,0:T(8,128)S(1)}, f32[1,128,1280]{2,1,0:T(8,128)S(1)}, u32[]{:S(2)}, u32[]{:S(2)}) %collective-permute-start.22) | collective-permute-done | bytes 655392 | tf_op jit(solution)/shard_map/ppermute | solution.py:37
  260.5 4.0 partial_sums.31
  264.6 4.7 peer_half.17.refs_5_
  273.5 27.6 %collective-permute-done.29.refs_4_.refs_1_ = f32[2,128,1280]{2,1,0:T(8,128)S(1)} collective-permute-done((f32[2,128,1280]{2,1,0:T(8,128)S(1)}, f32[2,128,1280]{2,1,0:T(8,128)S(1)}, u32[]{:S(2)}, u32[]{:S(2)}) %collective-permute-start.29) | collective-permute-done | bytes 1310752 | tf_op jit(solution)/shard_map/ppermute | solution.py:37
  306.7 8.0 %collective-permute-done.27.refs_3_ = f32[1,128,1280]{2,1,0:T(8,128)S(1)} collective-permute-done((f32[1,128,1280]{2,1,0:T(8,128)S(1)}, f32[1,128,1280]{2,1,0:T(8,128)S(1)}, u32[]{:S(2)}, u32[]{:S(2)}) %collective-permute-start.27) | collective-permute-done | bytes 655392 | tf_op jit(solution)/shard_map/ppermute | solution.py:37
  321.6 4.1 partial_sums.33
  325.6 3.9 peer_half.18.refs_5_
  333.6 27.6 %collective-permute-done.34.refs_4_.refs_1_ = f32[2,128,1280]{2,1,0:T(8,128)S(1)} collective-permute-done((f32[2,128,1280]{2,1,0:T(8,128)S(1)}, f32[2,128,1280]{2,1,0:T(8,128)S(1)}, u32[]{:S(2)}, u32[]{:S(2)}) %collective-permute-start.34) | collective-permute-done | bytes 1310752 | tf_op jit(solution)/shard_map/ppermute | solution.py:37
  367.4 8.7 %collective-permute-done.32.refs_3_ = f32[1,128,1280]{2,1,0:T(8,128)S(1)} collective-permute-done((f32[1,128,1280]{2,1,0:T(8,128)S(1)}, f32[1,128,1280]{2,1,0:T(8,128)S(1)}, u32[]{:S(2)}, u32[]{:S(2)}) %collective-permute-start.32) | collective-permute-done | bytes 655392 | tf_op jit(solution)/shard_map/ppermute | solution.py:37
  389.0 3.7 collective-permute-done.38.refs_1_
  394.7 25.6 %collective-permute-done.41.refs_3_ = f32[2,512]{1,0:T(2,128)S(1)} collective-permute-done((f32[2,512]{1,0:T(2,128)S(1)}, f32[2,512]{1,0:T(2,128)S(1)}, u32[]{:S(2)}, u32[]{:S(2)}) %collective-permute-start.41) | collective-permute-done | bytes 4128 | tf_op jit(solution)/shard_map/ppermute | solution.py:37
  428.1 7.9 %collective-permute-done.39.refs_1_ = f32[2,512]{1,0:T(2,128)S(1)} collective-permute-done((f32[2,512]{1,0:T(2,128)S(1)}, f32[2,512]{1,0:T(2,128)S(1)}, u32[]{:S(2)}, u32[]{:S(2)}) %collective-permute-start.39) | collective-permute-done | bytes 4128 | tf_op jit(solution)/shard_map/ppermute | solution.py:37
  446.8 5.6 %collective-permute-done.49.refs_4_.refs_1_ = f32[2,64,1280]{2,1,0:T(8,128)S(1)} collective-permute-done((f32[2,64,1280]{2,1,0:T(8,128)S(1)}, f32[2,64,1280]{2,1,0:T(8,128)S(1)}, u32[]{:S(2)}, u32[]{:S(2)}) %collective-permute-start.49) | collective-permute-done | bytes 655392 | tf_op jit(solution)/shard_map/ppermute | solution.py:37
  458.6 9.1 %collective-permute-done.47.refs_3_ = f32[1,128,1280]{2,1,0:T(8,128)S(1)} collective-permute-done((f32[1,128,1280]{2,1,0:T(8,128)S(1)}, f32[1,128,1280]{2,1,0:T(8,128)S(1)}, u32[]{:S(2)}, u32[]{:S(2)}) %collective-permute-start.47) | collective-permute-done | bytes 655392 | tf_op jit(solution)/shard_map/ppermute | solution.py:37
  472.2 8.3 %collective-permute-done.45.refs_4_.refs_1_ = f32[2,64,1280]{2,1,0:T(8,128)S(1)} collective-permute-done((f32[2,64,1280]{2,1,0:T(8,128)S(1)}, f32[2,64,1280]{2,1,0:T(8,128)S(1)}, u32[]{:S(2)}, u32[]{:S(2)}) %collective-permute-start.45) | collective-permute-done | bytes 655392 | tf_op jit(solution)/shard_map/ppermute | solution.py:37
  (316 shorter events, 194.5 us)
Async XLA Ops:
  89.2 45.8 %collective-permute-start.10 = (f32[2,4,128,1280]{3,2,1,0:T(8,128)}, f32[2,4,128,1280]{3,2,1,0:T(8,128)S(1)}, u32[]{:S(2)}, u32[]{:S(2)}) collective-permute-start(f32[2,4,128,1280]{3,2,1,0:T(8,128)} %peer_half.14.refs_5_), channel_id=1, source_target_pairs={{0,1},{1,0},{2,3},{3,2},{4,5},{5,4},{6,7},{7,6},{8,9},{9,8},{10,11... | collective-permute-start | bytes 15728648 | tf_op jit(solution)/shard_map/ppermute | solution.py:37
  89.3 31.7 %collective-permute-start.14 = (f32[2,128,1280]{2,1,0:T(8,128)S(1)}, f32[2,128,1280]{2,1,0:T(8,128)S(1)}, u32[]{:S(2)}, u32[]{:S(2)}) collective-permute-start(f32[2,128,1280]{2,1,0:T(8,128)S(1)} %copy-done.67), channel_id=1, source_target_pairs={{0,4},{1,5},{2,6},{3,7},{4,0},{5,1},{6,2},{7,3},{8,12},{9,13},{10,... | collective-permute-start | bytes 3932168 | tf_op jit(solution)/shard_map/ppermute | solution.py:37
  90.9 31.7 %collective-permute-start.13 = (f32[2,128,1280]{2,1,0:T(8,128)S(1)}, f32[2,128,1280]{2,1,0:T(8,128)S(1)}, u32[]{:S(2)}, u32[]{:S(2)}) collective-permute-start(f32[2,128,1280]{2,1,0:T(8,128)S(1)} %copy-done.40), channel_id=1, source_target_pairs={{0,2},{1,3},{2,0},{3,1},{4,6},{5,7},{6,4},{7,5},{8,10},{9,11},{10,... | collective-permute-start | bytes 3932168 | tf_op jit(solution)/shard_map/ppermute | solution.py:37
  91.4 40.8 %collective-permute-start.12 = (f32[1,96,1280]{2,1,0:T(8,128)S(1)}, f32[1,96,1280]{2,1,0:T(8,128)S(1)}, u32[]{:S(2)}, u32[]{:S(2)}) collective-permute-start(f32[1,96,1280]{2,1,0:T(8,128)S(1)} %get-tuple-element.96), channel_id=1, source_target_pairs={{0,2},{1,3},{2,0},{3,1},{4,6},{5,7},{6,4},{7,5},{8,10},{9,11},{10,... | collective-permute-start | bytes 1474568 | tf_op jit(solution)/shard_map/ppermute | solution.py:37
  92.9 39.3 %collective-permute-start.11 = (f32[1,96,1280]{2,1,0:T(8,128)S(1)}, f32[1,96,1280]{2,1,0:T(8,128)S(1)}, u32[]{:S(2)}, u32[]{:S(2)}) collective-permute-start(f32[1,96,1280]{2,1,0:T(8,128)S(1)} %get-tuple-element.93.refs_4_), channel_id=1, source_target_pairs={{0,4},{1,5},{2,6},{3,7},{4,0},{5,1},{6,2},{7,3},{8,12},{9,13},{10,... | collective-permute-start | bytes 1474568 | tf_op jit(solution)/shard_map/ppermute | solution.py:37
  146.3 49.8 %collective-permute-start.15 = (f32[2,4,128,1280]{3,2,1,0:T(8,128)}, f32[2,4,128,1280]{3,2,1,0:T(8,128)S(1)}, u32[]{:S(2)}, u32[]{:S(2)}) collective-permute-start(f32[2,4,128,1280]{3,2,1,0:T(8,128)} %peer_half.15.refs_5_), channel_id=1, source_target_pairs={{0,1},{1,0},{2,3},{3,2},{4,5},{5,4},{6,7},{7,6},{8,9},{9,8},{10,11... | collective-permute-start | bytes 15728648 | tf_op jit(solution)/shard_map/ppermute | solution.py:37
  146.3 31.7 %collective-permute-start.19 = (f32[2,128,1280]{2,1,0:T(8,128)S(1)}, f32[2,128,1280]{2,1,0:T(8,128)S(1)}, u32[]{:S(2)}, u32[]{:S(2)}) collective-permute-start(f32[2,128,1280]{2,1,0:T(8,128)S(1)} %copy-done.63), channel_id=1, source_target_pairs={{0,4},{1,5},{2,6},{3,7},{4,0},{5,1},{6,2},{7,3},{8,12},{9,13},{10,... | collective-permute-start | bytes 3932168 | tf_op jit(solution)/shard_map/ppermute | solution.py:37
  146.8 31.7 %collective-permute-start.18 = (f32[2,128,1280]{2,1,0:T(8,128)S(1)}, f32[2,128,1280]{2,1,0:T(8,128)S(1)}, u32[]{:S(2)}, u32[]{:S(2)}) collective-permute-start(f32[2,128,1280]{2,1,0:T(8,128)S(1)} %copy-done.36), channel_id=1, source_target_pairs={{0,2},{1,3},{2,0},{3,1},{4,6},{5,7},{6,4},{7,5},{8,10},{9,11},{10,... | collective-permute-start | bytes 3932168 | tf_op jit(solution)/shard_map/ppermute | solution.py:37
  147.4 44.3 %collective-permute-start.17 = (f32[1,128,1280]{2,1,0:T(8,128)S(1)}, f32[1,128,1280]{2,1,0:T(8,128)S(1)}, u32[]{:S(2)}, u32[]{:S(2)}) collective-permute-start(f32[1,128,1280]{2,1,0:T(8,128)S(1)} %copy-done.71), channel_id=1, source_target_pairs={{0,2},{1,3},{2,0},{3,1},{4,6},{5,7},{6,4},{7,5},{8,10},{9,11},{10,... | collective-permute-start | bytes 1966088 | tf_op jit(solution)/shard_map/ppermute | solution.py:37
  148.9 42.9 %collective-permute-start.16 = (f32[1,128,1280]{2,1,0:T(8,128)S(1)}, f32[1,128,1280]{2,1,0:T(8,128)S(1)}, u32[]{:S(2)}, u32[]{:S(2)}) collective-permute-start(f32[1,128,1280]{2,1,0:T(8,128)S(1)} %copy-done.55), channel_id=1, source_target_pairs={{0,4},{1,5},{2,6},{3,7},{4,0},{5,1},{6,2},{7,3},{8,12},{9,13},{10,... | collective-permute-start | bytes 1966088 | tf_op jit(solution)/shard_map/ppermute | solution.py:37
  207.3 51.0 %collective-permute-start.20 = (f32[2,4,128,1280]{3,2,1,0:T(8,128)}, f32[2,4,128,1280]{3,2,1,0:T(8,128)S(1)}, u32[]{:S(2)}, u32[]{:S(2)}) collective-permute-start(f32[2,4,128,1280]{3,2,1,0:T(8,128)} %peer_half.16.refs_5_), channel_id=1, source_target_pairs={{0,1},{1,0},{2,3},{3,2},{4,5},{5,4},{6,7},{7,6},{8,9},{9,8},{10,11... | collective-permute-start | bytes 15728648 | tf_op jit(solution)/shard_map/ppermute | solution.py:37
  207.3 31.7 %collective-permute-start.24 = (f32[2,128,1280]{2,1,0:T(8,128)S(1)}, f32[2,128,1280]{2,1,0:T(8,128)S(1)}, u32[]{:S(2)}, u32[]{:S(2)}) collective-permute-start(f32[2,128,1280]{2,1,0:T(8,128)S(1)} %copy-done.64), channel_id=1, source_target_pairs={{0,4},{1,5},{2,6},{3,7},{4,0},{5,1},{6,2},{7,3},{8,12},{9,13},{10,... | collective-permute-start | bytes 3932168 | tf_op jit(solution)/shard_map/ppermute | solution.py:37
  208.9 31.7 %collective-permute-start.23 = (f32[2,128,1280]{2,1,0:T(8,128)S(1)}, f32[2,128,1280]{2,1,0:T(8,128)S(1)}, u32[]{:S(2)}, u32[]{:S(2)}) collective-permute-start(f32[2,128,1280]{2,1,0:T(8,128)S(1)} %copy-done.37), channel_id=1, source_target_pairs={{0,2},{1,3},{2,0},{3,1},{4,6},{5,7},{6,4},{7,5},{8,10},{9,11},{10,... | collective-permute-start | bytes 3932168 | tf_op jit(solution)/shard_map/ppermute | solution.py:37
  209.4 44.3 %collective-permute-start.22 = (f32[1,128,1280]{2,1,0:T(8,128)S(1)}, f32[1,128,1280]{2,1,0:T(8,128)S(1)}, u32[]{:S(2)}, u32[]{:S(2)}) collective-permute-start(f32[1,128,1280]{2,1,0:T(8,128)S(1)} %copy-done.72), channel_id=1, source_target_pairs={{0,2},{1,3},{2,0},{3,1},{4,6},{5,7},{6,4},{7,5},{8,10},{9,11},{10,... | collective-permute-start | bytes 1966088 | tf_op jit(solution)/shard_map/ppermute | solution.py:37
  210.9 42.9 %collective-permute-start.21 = (f32[1,128,1280]{2,1,0:T(8,128)S(1)}, f32[1,128,1280]{2,1,0:T(8,128)S(1)}, u32[]{:S(2)}, u32[]{:S(2)}) collective-permute-start(f32[1,128,1280]{2,1,0:T(8,128)S(1)} %copy-done.42), channel_id=1, source_target_pairs={{0,4},{1,5},{2,6},{3,7},{4,0},{5,1},{6,2},{7,3},{8,12},{9,13},{10,... | collective-permute-start | bytes 1966088 | tf_op jit(solution)/shard_map/ppermute | solution.py:37
  269.3 49.9 %collective-permute-start.25 = (f32[2,4,128,1280]{3,2,1,0:T(8,128)}, f32[2,4,128,1280]{3,2,1,0:T(8,128)S(1)}, u32[]{:S(2)}, u32[]{:S(2)}) collective-permute-start(f32[2,4,128,1280]{3,2,1,0:T(8,128)} %peer_half.17.refs_5_), channel_id=1, source_target_pairs={{0,1},{1,0},{2,3},{3,2},{4,5},{5,4},{6,7},{7,6},{8,9},{9,8},{10,11... | collective-permute-start | bytes 15728648 | tf_op jit(solution)/shard_map/ppermute | solution.py:37
  269.3 31.7 %collective-permute-start.29 = (f32[2,128,1280]{2,1,0:T(8,128)S(1)}, f32[2,128,1280]{2,1,0:T(8,128)S(1)}, u32[]{:S(2)}, u32[]{:S(2)}) collective-permute-start(f32[2,128,1280]{2,1,0:T(8,128)S(1)} %copy-done.65), channel_id=1, source_target_pairs={{0,4},{1,5},{2,6},{3,7},{4,0},{5,1},{6,2},{7,3},{8,12},{9,13},{10,... | collective-permute-start | bytes 3932168 | tf_op jit(solution)/shard_map/ppermute | solution.py:37
  269.9 31.7 %collective-permute-start.28 = (f32[2,128,1280]{2,1,0:T(8,128)S(1)}, f32[2,128,1280]{2,1,0:T(8,128)S(1)}, u32[]{:S(2)}, u32[]{:S(2)}) collective-permute-start(f32[2,128,1280]{2,1,0:T(8,128)S(1)} %copy-done.38), channel_id=1, source_target_pairs={{0,2},{1,3},{2,0},{3,1},{4,6},{5,7},{6,4},{7,5},{8,10},{9,11},{10,... | collective-permute-start | bytes 3932168 | tf_op jit(solution)/shard_map/ppermute | solution.py:37
  270.4 44.4 %collective-permute-start.27 = (f32[1,128,1280]{2,1,0:T(8,128)S(1)}, f32[1,128,1280]{2,1,0:T(8,128)S(1)}, u32[]{:S(2)}, u32[]{:S(2)}) collective-permute-start(f32[1,128,1280]{2,1,0:T(8,128)S(1)} %copy-done.73), channel_id=1, source_target_pairs={{0,2},{1,3},{2,0},{3,1},{4,6},{5,7},{6,4},{7,5},{8,10},{9,11},{10,... | collective-permute-start | bytes 1966088 | tf_op jit(solution)/shard_map/ppermute | solution.py:37
  271.9 42.9 %collective-permute-start.26 = (f32[1,128,1280]{2,1,0:T(8,128)S(1)}, f32[1,128,1280]{2,1,0:T(8,128)S(1)}, u32[]{:S(2)}, u32[]{:S(2)}) collective-permute-start(f32[1,128,1280]{2,1,0:T(8,128)S(1)} %copy-done.43), channel_id=1, source_target_pairs={{0,4},{1,5},{2,6},{3,7},{4,0},{5,1},{6,2},{7,3},{8,12},{9,13},{10,... | collective-permute-start | bytes 1966088 | tf_op jit(solution)/shard_map/ppermute | solution.py:37
  329.5 51.0 %collective-permute-start.30 = (f32[2,4,64,1280]{3,2,1,0:T(8,128)}, f32[2,4,64,1280]{3,2,1,0:T(8,128)S(1)}, u32[]{:S(2)}, u32[]{:S(2)}) collective-permute-start(f32[2,4,64,1280]{3,2,1,0:T(8,128)} %peer_half.18.refs_5_), channel_id=1, source_target_pairs={{0,1},{1,0},{2,3},{3,2},{4,5},{5,4},{6,7},{7,6},{8,9},{9,8},{10,11... | collective-permute-start | bytes 7864328 | tf_op jit(solution)/shard_map/ppermute | solution.py:37
  329.5 31.7 %collective-permute-start.34 = (f32[2,128,1280]{2,1,0:T(8,128)S(1)}, f32[2,128,1280]{2,1,0:T(8,128)S(1)}, u32[]{:S(2)}, u32[]{:S(2)}) collective-permute-start(f32[2,128,1280]{2,1,0:T(8,128)S(1)} %copy-done.66), channel_id=1, source_target_pairs={{0,4},{1,5},{2,6},{3,7},{4,0},{5,1},{6,2},{7,3},{8,12},{9,13},{10,... | collective-permute-start | bytes 3932168 | tf_op jit(solution)/shard_map/ppermute | solution.py:37
  331.2 31.6 %collective-permute-start.33 = (f32[2,128,1280]{2,1,0:T(8,128)S(1)}, f32[2,128,1280]{2,1,0:T(8,128)S(1)}, u32[]{:S(2)}, u32[]{:S(2)}) collective-permute-start(f32[2,128,1280]{2,1,0:T(8,128)S(1)} %copy-done.39), channel_id=1, source_target_pairs={{0,2},{1,3},{2,0},{3,1},{4,6},{5,7},{6,4},{7,5},{8,10},{9,11},{10,... | collective-permute-start | bytes 3932168 | tf_op jit(solution)/shard_map/ppermute | solution.py:37
  331.6 44.4 %collective-permute-start.32 = (f32[1,128,1280]{2,1,0:T(8,128)S(1)}, f32[1,128,1280]{2,1,0:T(8,128)S(1)}, u32[]{:S(2)}, u32[]{:S(2)}) collective-permute-start(f32[1,128,1280]{2,1,0:T(8,128)S(1)} %copy-done.74), channel_id=1, source_target_pairs={{0,2},{1,3},{2,0},{3,1},{4,6},{5,7},{6,4},{7,5},{8,10},{9,11},{10,... | collective-permute-start | bytes 1966088 | tf_op jit(solution)/shard_map/ppermute | solution.py:37
  333.2 42.9 %collective-permute-start.31 = (f32[1,128,1280]{2,1,0:T(8,128)S(1)}, f32[1,128,1280]{2,1,0:T(8,128)S(1)}, u32[]{:S(2)}, u32[]{:S(2)}) collective-permute-start(f32[1,128,1280]{2,1,0:T(8,128)S(1)} %copy-done.44), channel_id=1, source_target_pairs={{0,4},{1,5},{2,6},{3,7},{4,0},{5,1},{6,2},{7,3},{8,12},{9,13},{10,... | collective-permute-start | bytes 1966088 | tf_op jit(solution)/shard_map/ppermute | solution.py:37
  387.7 55.6 %collective-permute-start.35 = (f32[2,4,64,1280]{3,2,1,0:T(8,128)S(1)}, f32[2,4,64,1280]{3,2,1,0:T(8,128)S(1)}, u32[]{:S(2)}, u32[]{:S(2)}) collective-permute-start(f32[2,4,64,1280]{3,2,1,0:T(8,128)S(1)} %peer_half.19.refs_5_), channel_id=1, source_target_pairs={{0,1},{1,0},{2,3},{3,2},{4,5},{5,4},{6,7},{7,6},{8,9},{9,8},{10,11... | collective-permute-start | bytes 7864328 | tf_op jit(solution)/shard_map/ppermute | solution.py:37
  387.8 33.5 %collective-permute-start.43 = (f32[2,128,1280]{2,1,0:T(8,128)S(1)}, f32[2,128,1280]{2,1,0:T(8,128)S(1)}, u32[]{:S(2)}, u32[]{:S(2)}) collective-permute-start(f32[2,128,1280]{2,1,0:T(8,128)S(1)} %copy-done.62), channel_id=1, source_target_pairs={{0,4},{1,5},{2,6},{3,7},{4,0},{5,1},{6,2},{7,3},{8,12},{9,13},{10,... | collective-permute-start | bytes 3932168 | tf_op jit(solution)/shard_map/ppermute | solution.py:37
  388.4 34.5 %collective-permute-start.42 = (f32[2,128,1280]{2,1,0:T(8,128)S(1)}, f32[2,128,1280]{2,1,0:T(8,128)S(1)}, u32[]{:S(2)}, u32[]{:S(2)}) collective-permute-start(f32[2,128,1280]{2,1,0:T(8,128)S(1)} %copy-done.35), channel_id=1, source_target_pairs={{0,2},{1,3},{2,0},{3,1},{4,6},{5,7},{6,4},{7,5},{8,10},{9,11},{10,... | collective-permute-start | bytes 3932168 | tf_op jit(solution)/shard_map/ppermute | solution.py:37
  421.4 31.0 %collective-permute-start.49 = (f32[2,64,1280]{2,1,0:T(8,128)S(1)}, f32[2,64,1280]{2,1,0:T(8,128)S(1)}, u32[]{:S(2)}, u32[]{:S(2)}) collective-permute-start(f32[2,64,1280]{2,1,0:T(8,128)S(1)} %copy-done.68), channel_id=1, source_target_pairs={{0,4},{1,5},{2,6},{3,7},{4,0},{5,1},{6,2},{7,3},{8,12},{9,13},{10,... | collective-permute-start | bytes 1966088 | tf_op jit(solution)/shard_map/ppermute | solution.py:37
  437.9 30.2 %collective-permute-start.46 = (f32[1,128,1280]{2,1,0:T(8,128)S(1)}, f32[1,128,1280]{2,1,0:T(8,128)S(1)}, u32[]{:S(2)}, u32[]{:S(2)}) collective-permute-start(f32[1,128,1280]{2,1,0:T(8,128)S(1)} %copy-done.51), channel_id=1, source_target_pairs={{0,4},{1,5},{2,6},{3,7},{4,0},{5,1},{6,2},{7,3},{8,12},{9,13},{10,... | collective-permute-start | bytes 1966088 | tf_op jit(solution)/shard_map/ppermute | solution.py:37
  445.2 35.3 %collective-permute-start.45 = (f32[2,64,1280]{2,1,0:T(8,128)S(1)}, f32[2,64,1280]{2,1,0:T(8,128)S(1)}, u32[]{:S(2)}, u32[]{:S(2)}) collective-permute-start(f32[2,64,1280]{2,1,0:T(8,128)S(1)} %get-tuple-element.139), channel_id=1, source_target_pairs={{0,4},{1,5},{2,6},{3,7},{4,0},{5,1},{6,2},{7,3},{8,12},{9,13},{10,... | collective-permute-start | bytes 1966088 | tf_op jit(solution)/shard_map/ppermute | solution.py:37
  457.7 31.0 %collective-permute-start.53 = (f32[1,64,1280]{2,1,0:T(8,128)}, f32[1,64,1280]{2,1,0:T(8,128)S(1)}, u32[]{:S(2)}, u32[]{:S(2)}) collective-permute-start(f32[1,64,1280]{2,1,0:T(8,128)} %get-tuple-element.148), channel_id=1, source_target_pairs={{0,2},{1,3},{2,0},{3,1},{4,6},{5,7},{6,4},{7,5},{8,10},{9,11},{10,... | collective-permute-start | bytes 983048 | tf_op jit(solution)/shard_map/ppermute | solution.py:37
  (115 other events, 990.2 us)
